TPU v7x, 16 devices: a whole 2x2x2 slice. The times are simulated.
16 devices in a mesh: fsdp: 2 (over z), ep: 8 (over y, x, core).
Axes of the slice: x: 2, y: 2, z: 2, core: 2. Of those that a mesh axis runs over, the one named last changes fastest.
Arguments:
- layer_in: bfloat16 [32768, 1536], P(('fsdp', 'ep'))
- out_grad: bfloat16 [32768, 1536], P(('fsdp', 'ep'))
- expert_ids: int32 [32768, 8], P(('fsdp', 'ep'))
- gate_vals: float32 [32768, 8], P(('fsdp', 'ep'))
- w_one: bfloat16 [40, 1536, 512], P('ep', 'fsdp')
- w_two: bfloat16 [40, 512, 1536], P('ep', None, 'fsdp')
- w_three: bfloat16 [40, 1536, 512], P('ep', 'fsdp')
Outputs:
- output 1: bfloat16 [32768, 1536], P(('fsdp', 'ep'))
- output 2: float32 [32768, 8], P(('fsdp', 'ep'))
- output 3: float32 [40, 1536, 512], P('ep', 'fsdp')
- output 4: float32 [40, 512, 1536], P('ep', None, 'fsdp')
- output 5: float32 [40, 1536, 512], P('ep', 'fsdp')
All inputs are finite; a program needn't handle non-finite values.
Results may differ from a plain program's by a relative error of at most 0.00144.
Values are sent between devices in bfloat16 or wider.
A program may use at most 1 GiB of HBM per device.

v0:
```python
import jax
import jax.numpy as jnp
from jax import lax
from jax.sharding import PartitionSpec as P


def capacity_of(tok_dev, top_k, experts):
    return max(8, ((tok_dev * top_k * 5) // (4 * experts) + 7) // 8 * 8)


def route_slots(expert_ids, experts, capacity):
    flat_ids = expert_ids.reshape(-1)
    onehot = (flat_ids[:, None] == jnp.arange(experts, dtype=jnp.int32)[None, :]).astype(jnp.int32)
    before = jnp.cumsum(onehot, axis=0) - onehot
    position = jnp.sum(before * onehot, axis=1)
    return jnp.where(position < capacity, flat_ids * capacity + position, experts * capacity)


def slot_sources(slot_of, gate_vals, tok_dev, places):
    top_k = gate_vals.shape[-1]
    token_of = jnp.arange(slot_of.shape[0], dtype=jnp.int32) // top_k
    source = jnp.full((places,), tok_dev, jnp.int32).at[slot_of].set(token_of, mode="drop")
    slot_gate = jnp.zeros((places,), jnp.float32).at[slot_of].set(gate_vals.reshape(-1), mode="drop")
    return source, slot_gate


def take_rows(rows, row_index):
    return jnp.take(rows, row_index, axis=0, mode="fill", fill_value=0)


def expert_grads(x_rows, dy_rows, gate_rows, w_one, w_two, w_three):
    h_one = jnp.einsum("pecd,edf->pecf", x_rows, w_one, preferred_element_type=jnp.float32)
    h_three = jnp.einsum("pecd,edf->pecf", x_rows, w_three, preferred_element_type=jnp.float32)
    sig_one = jax.nn.sigmoid(h_one)
    silu_one = h_one * sig_one
    act_bf = (silu_one * h_three).astype(jnp.bfloat16)
    y_rows = jnp.einsum("pecf,efd->pecd", act_bf, w_two, preferred_element_type=jnp.float32)
    gate_grad = jnp.sum(dy_rows.astype(jnp.float32) * y_rows, axis=-1)
    g_rows = (gate_rows[..., None] * dy_rows.astype(jnp.float32)).astype(jnp.bfloat16)
    d_act = jnp.einsum("pecd,efd->pecf", g_rows, w_two, preferred_element_type=jnp.float32)
    dh_one = (d_act * h_three * sig_one * (1.0 + h_one * (1.0 - sig_one))).astype(jnp.bfloat16)
    dh_three = (d_act * silu_one).astype(jnp.bfloat16)
    dx_rows = (jnp.einsum("pecf,edf->pecd", dh_one, w_one, preferred_element_type=jnp.float32) + jnp.einsum("pecf,edf->pecd", dh_three, w_three, preferred_element_type=jnp.float32)).astype(jnp.bfloat16)
    grad_one = jnp.einsum("pecd,pecf->edf", x_rows, dh_one, preferred_element_type=jnp.float32)
    grad_three = jnp.einsum("pecd,pecf->edf", x_rows, dh_three, preferred_element_type=jnp.float32)
    grad_two = jnp.einsum("pecf,pecd->efd", act_bf, g_rows, preferred_element_type=jnp.float32)
    return dx_rows, gate_grad, grad_one, grad_two, grad_three


def solution(mesh):
    ep_size = mesh.shape["ep"]
    tok_spec = P(("fsdp", "ep"), None)
    up_spec = P("ep", "fsdp", None)
    down_spec = P("ep", None, "fsdp")

    def per_device(layer_in, out_grad, expert_ids, gate_vals, w_one, w_two, w_three):
        tok_dev, hidden = layer_in.shape
        top_k = expert_ids.shape[1]
        local_experts = w_one.shape[0]
        experts = local_experts * ep_size
        capacity = capacity_of(tok_dev, top_k, experts)
        places = experts * capacity
        slot_of = route_slots(expert_ids, experts, capacity)
        source, slot_gate = slot_sources(slot_of, gate_vals, tok_dev, places)
        send_shape = (ep_size, local_experts, capacity, hidden)
        x_send = take_rows(layer_in, source).reshape(send_shape)
        dy_send = take_rows(out_grad, source).reshape(send_shape)
        gate_send = slot_gate.reshape(ep_size, local_experts, capacity)
        x_rows = lax.all_to_all(x_send, "ep", 0, 0, tiled=True)
        dy_rows = lax.all_to_all(dy_send, "ep", 0, 0, tiled=True)
        gate_rows = lax.all_to_all(gate_send, "ep", 0, 0, tiled=True)
        w_one_full = lax.all_gather(w_one, "fsdp", axis=1, tiled=True)
        w_three_full = lax.all_gather(w_three, "fsdp", axis=1, tiled=True)
        w_two_full = lax.all_gather(w_two, "fsdp", axis=2, tiled=True)
        dx_rows, gate_grad, grad_one, grad_two, grad_three = expert_grads(x_rows, dy_rows, gate_rows, w_one_full, w_two_full, w_three_full)
        dx_back = lax.all_to_all(dx_rows, "ep", 0, 0, tiled=True).reshape(places, hidden)
        gate_back = lax.all_to_all(gate_grad, "ep", 0, 0, tiled=True).reshape(places)
        dx_pick = take_rows(dx_back, slot_of).reshape(tok_dev, top_k, hidden)
        in_grad = jnp.sum(dx_pick, axis=1, dtype=jnp.float32).astype(jnp.bfloat16)
        gate_out = take_rows(gate_back, slot_of).reshape(tok_dev, top_k)
        grad_one = lax.psum_scatter(grad_one, "fsdp", scatter_dimension=1, tiled=True)
        grad_three = lax.psum_scatter(grad_three, "fsdp", scatter_dimension=1, tiled=True)
        grad_two = lax.psum_scatter(grad_two, "fsdp", scatter_dimension=2, tiled=True)
        return in_grad, gate_out, grad_one, grad_two, grad_three

    return jax.shard_map(per_device, mesh=mesh, in_specs=(tok_spec, tok_spec, tok_spec, tok_spec, up_spec, down_spec, up_spec), out_specs=(tok_spec, tok_spec, up_spec, down_spec, up_spec), check_vma=False)
```

profile of v0, /device:TPU:0, one launch (start us, length us, event | category | flops | bytes accessed | tf_op | source)
XLA Modules:
  0.0 3469.7 jit_solution(13427629694647927627)
XLA Ops:
  7.2 1.2 copy.46
  8.3 0.5 eq.29
  8.9 0.5 eq.25
  9.4 0.1 broadcast_multiply_fusion
  9.4 0.1 copy.48
  9.5 0.5 mul.54
  10.1 1.2 copy.51
  11.2 0.5 reshape.146
  11.7 0.3 fusion.44
  12.1 1.5 copy-done.2
  13.6 0.3 reduce-window.9
  13.9 3.4 broadcast_add_fusion
  17.3 3.4 copy.49
  20.7 3.9 fusion.43
  24.7 0.6 copy-done.3
  25.3 0.1 compare_select_fusion.1
  25.4 60.4 %scatter_custom_fusion = f32[20480]{0:T(1024)S(1)} fusion(s32[16384]{0:T(1024)S(1)} %bitcast.112, f32[16384]{0:T(1024)S(1)} %reshape.146, f32[]{:T(128)} %constant.65.clone.1), kind=kCustom, calls=%fused_computation.79 | custom fusion | bytes 81924 | tf_op jit(solution)/shard_map/scatter | solution.py:23
  85.8 0.7 reshape.105
  86.4 5.5 all-to-all-start
  91.9 60.7 %scatter_custom_fusion.1 = s32[20480]{0:T(1024)S(1)} fusion(s32[16384]{0:T(1024)S(1)} %bitcast.113, s32[16384]{0:T(1024)S(1)} %add_select_fusion, s32[]{:T(128)} %constant.66.clone.1), kind=kCustom, calls=%fused_computation.77 | custom fusion | bytes 81924 | tf_op jit(solution)/shard_map/scatter | solution.py:22
  152.6 0.6 compare_and_fusion.1
  153.2 125.1 %gather_fusion.3 = bf16[20480,1536]{1,0:T(8,128)(2,1)} fusion(bf16[2048,1536]{1,0:T(8,128)(2,1)} %param.9, s32[20480]{0:T(1024)S(1)} %fusion.47), kind=kCustom, calls=%fused_computation.1.clone | custom fusion | bytes 125911040 | tf_op jit(solution)/shard_map/jit(_take)/gather | solution.py:28
  278.3 125.0 %gather_fusion.2 = bf16[20480,1536]{1,0:T(8,128)(2,1)} fusion(bf16[2048,1536]{1,0:T(8,128)(2,1)} %param.10, s32[20480]{0:T(1024)S(1)} %fusion.47), kind=kCustom, calls=%fused_computation.clone | custom fusion | bytes 125911040 | tf_op jit(solution)/shard_map/jit(_take)/gather | solution.py:28
  403.3 82.2 %broadcast_select_fusion.1 = (bf16[20480,1536]{1,0:T(8,128)(2,1)}, bf16[20480,1536]{1,0:T(8,128)(2,1)}) fusion(bf16[20480,1536]{1,0:T(8,128)(2,1)} %gather_fusion.2, pred[20480]{0:T(1024)(128)(4,1)S(1)} %copy-done.7, bf16[20480,1536]{1,0:T(8,128)(2,1)} %gather_fusion.3), kind=kLoop, calls=%fused_computation.12 | loop fusion | flops 62914560 | bytes 251678720 | tf_op jit(solution)/shard_map/jit(_take)/select_n | solution.py:28
  485.5 695.3 %all_to_all.25 = bf16[8,5,512,1536]{3,2,1,0:T(8,128)(2,1)} all-to-all(bf16[8,5,512,1536]{3,2,1,0:T(8,128)(2,1)} %bitcast.109), channel_id=1, replica_groups=mesh['fsdp'=2,'ep'=8] {'ep'}, dimensions={0} | all-to-all | bytes 125829120 | tf_op jit(solution)/shard_map/all_to_all | solution.py:69
  1180.9 9.5 all-to-all-start.1
  1190.4 0.0 all-gather.8.cloned.1.call-start
  1190.4 0.7 all-gather.8.cloned.1.call-update
  1191.1 0.0 all-gather.4.cloned.1.call-start
  1191.1 0.7 all-gather.4.cloned.1.call-update
  1191.8 0.0 all-gather.6.cloned.1.call-start
  1191.9 0.7 all-gather.6.cloned.1.call-update
  1192.6 0.6 reduce-scatter.6.cloned.1.call-start
  1193.2 1.0 copy.52
  1194.1 97.5 %all-gather.8.cloned.1.call-done = bf16[5,1536,512]{2,1,0:T(8,128)(2,1)} async-done(((bf16[5,768,512]{2,1,0:T(8,128)(2,1)}), bf16[5,1536,512]{2,1,0:T(8,128)(2,1)}) %all-gather.8.cloned.1.call-update) | async-done | bytes 7864336 | tf_op jit(solution)/shard_map/all_gather | solution.py:72
  1291.6 45.4 %fusion.2 = f32[5,8,512,512]{3,2,1,0:T(8,128)} fusion(bf16[8,5,512,1536]{3,2,1,0:T(8,128)(2,1)} %all_to_all.25, bf16[5,1536,512]{2,1,0:T(8,128)(2,1)} %all-gather.8.cloned.1.call-done), kind=kOutput, calls=%fused_computation.13 | convolution fusion | flops 32212254720 | bytes 112721920 | tf_op jit(solution)/shard_map/pecd,edf->pecf/dot_general | solution.py:32
  1337.1 53.3 %all-gather.4.cloned.1.call-done = bf16[5,512,1536]{2,1,0:T(8,128)(2,1)} async-done(((bf16[5,512,768]{2,1,0:T(8,128)(2,1)}), bf16[5,512,1536]{2,1,0:T(8,128)(2,1)}) %all-gather.4.cloned.1.call-update) | async-done | bytes 7864336 | tf_op jit(solution)/shard_map/all_gather | solution.py:74
  1390.4 478.8 %all-to-all-done.1 = bf16[8,5,512,1536]{3,2,1,0:T(8,128)(2,1)} async-done(((bf16[8,5,512,1536]{3,2,1,0:T(8,128)(2,1)}), bf16[8,5,512,1536]{3,2,1,0:T(8,128)(2,1)}, u32[]{:S(2)}, u32[]{:S(2)}) %all-to-all-start.1) | async-done | bytes 62914592 | tf_op jit(solution)/shard_map/all_to_all | solution.py:70
  1869.2 45.9 %fusion.10 = f32[5,8,512,512]{3,2,1,0:T(8,128)} fusion(f32[8,5,512]{2,0,1:T(8,128)S(1)} %copy.52, bf16[8,5,512,1536]{3,2,1,0:T(8,128)(2,1)} %all-to-all-done.1, bf16[5,512,1536]{2,1,0:T(8,128)(2,1)} %all-gather.4.cloned.1.call-done), kind=kOutput, calls=%fused_computation.21 | convolution fusion | flops 32306626560 | bytes 112803840 | tf_op jit(solution)/shard_map/pecd,efd->pecf/dot_general | solution.py:40
  1915.1 79.3 %fusion.19 = (bf16[8,5,512,512]{3,2,0,1:T(8,128)(2,1)}, bf16[8,5,512,512]{3,2,0,1:T(8,128)(2,1)}, bf16[8,5,512,512]{3,2,0,1:T(8,128)(2,1)}) fusion(f32[5,8,512,512]{3,2,1,0:T(8,128)} %fusion.2, f32[5,8,512,512]{3,2,1,0:T(8,128)} %fusion.10, bf16[5,1536,512]{2,1,0:T(8,128)(2,1)} %all-gather.6.cloned.1.call-done, bf16[8,5,512,1536]{3,2,1,0:T(8,128)(2,1)} %all_to_all.25), kind=kOutput, calls=%fused_computation.34 | convolution fusion | flops 32369541120 | bytes 217579520 | tf_op jit(solution)/shard_map/pecd,edf->pecf/dot_general | solution.py:33
  1994.4 42.8 %fusion.38 = f32[5,512,1536]{2,1,0:T(8,128)} fusion(bf16[8,5,512,512]{3,2,0,1:T(8,128)(2,1)} %get-tuple-element.23, f32[8,5,512]{2,0,1:T(8,128)S(1)} %copy.52, bf16[8,5,512,1536]{3,2,1,0:T(8,128)(2,1)} %all-to-all-done.1), kind=kOutput, calls=%fused_computation.50 | convolution fusion | flops 32306626560 | bytes 99696640 | tf_op jit(solution)/shard_map/pecf,pecd->efd/dot_general | solution.py:46
  2037.2 0.0 reduce-scatter.6.cloned.1.call-update
  2037.2 41.1 %fusion.1 = f32[8,5,512]{2,0,1:T(8,128)S(1)} fusion(bf16[8,5,512,512]{3,2,0,1:T(8,128)(2,1)} %get-tuple-element.23, bf16[8,5,512,1536]{3,2,1,0:T(8,128)(2,1)} %all-to-all-done.1, bf16[5,512,1536]{2,1,0:T(8,128)(2,1)} %all-gather.4.cloned.1.call-done), kind=kOutput, calls=%fused_computation.9 | convolution fusion | flops 32306606080 | bytes 91832320 | tf_op jit(solution)/shard_map/pecf,efd->pecd/dot_general | solution.py:37
  2078.3 0.7 copy.57
  2079.1 4.0 all-to-all-start.4
  2083.1 0.0 reduce-scatter.8.cloned.1.call-start
  2083.1 44.1 %fusion.35 = f32[5,1536,512]{2,1,0:T(8,128)} fusion(bf16[8,5,512,1536]{3,2,1,0:T(8,128)(2,1)} %all_to_all.25, bf16[8,5,512,512]{3,2,0,1:T(8,128)(2,1)} %get-tuple-element.25), kind=kOutput, calls=%fused_computation.49 | convolution fusion | flops 32212254720 | bytes 99614720 | tf_op jit(solution)/shard_map/pecd,pecf->edf/dot_general | solution.py:45
  2127.2 0.0 reduce-scatter.8.cloned.1.call-update
  2127.3 55.1 %fusion.25 = f32[5,8,512,1536]{3,2,1,0:T(8,128)} fusion(bf16[8,5,512,512]{3,2,0,1:T(8,128)(2,1)} %get-tuple-element.24, bf16[5,1536,512]{2,1,0:T(8,128)(2,1)} %all-gather.8.cloned.1.call-done), kind=kOutput, calls=%fused_computation.41 | convolution fusion | flops 32212254720 | bytes 154664960 | tf_op jit(solution)/shard_map/pecf,edf->pecd/dot_general | solution.py:43
  2182.4 71.1 %fusion.6 = bf16[8,5,512,1536]{3,2,0,1:T(8,128)(2,1)} fusion(f32[5,8,512,1536]{3,2,1,0:T(8,128)} %fusion.25, bf16[8,5,512,512]{3,2,0,1:T(8,128)(2,1)} %get-tuple-element.25, bf16[5,1536,512]{2,1,0:T(8,128)(2,1)} %all-gather.6.cloned.1.call-done), kind=kOutput, calls=%fused_computation.17 | convolution fusion | flops 32275169280 | bytes 217579520 | tf_op jit(solution)/shard_map/pecf,edf->pecd/dot_general | solution.py:43
  2253.5 42.3 %copy.56 = bf16[8,5,512,1536]{3,2,1,0:T(8,128)(2,1)} copy(bf16[8,5,512,1536]{3,2,0,1:T(8,128)(2,1)} %fusion.6) | data formatting | bytes 125829120 | tf_op jit(solution)/shard_map/convert_element_type | solution.py:43
  2295.8 9.5 all-to-all-start.3
  2305.3 0.0 reduce-scatter.4.cloned.1.call-start
  2305.3 44.4 %fusion.32 = f32[5,1536,512]{2,1,0:T(8,128)} fusion(bf16[8,5,512,1536]{3,2,1,0:T(8,128)(2,1)} %all_to_all.25, bf16[8,5,512,512]{3,2,0,1:T(8,128)(2,1)} %get-tuple-element.24), kind=kOutput, calls=%fused_computation.48 | convolution fusion | flops 32212254720 | bytes 99614720 | tf_op jit(solution)/shard_map/pecd,pecf->edf/dot_general | solution.py:44
  2349.7 0.0 reduce-scatter.4.cloned.1.call-update
  2349.8 0.6 reduce_sum.35
  2350.4 0.9 reshape.109
  2351.3 90.5 %gather_fusion.1 = f32[16384]{0:T(1024)S(1)} fusion(f32[20480]{0:T(1024)S(1)} %reshape.109, s32[16384]{0:T(1024)S(1)} %broadcast_clamp_fusion), kind=kCustom, calls=%fused_computation.3 | custom fusion | bytes 196608 | tf_op jit(solution)/shard_map/jit(_take)/gather | solution.py:28
  2441.8 0.6 gather.18
  2442.4 1.4 broadcast_select_fusion.2
  2443.8 2.2 copy.63
  2446.0 538.1 %all-to-all-done.3 = bf16[8,5,512,1536]{3,2,1,0:T(8,128)(2,1)} async-done(((bf16[8,5,512,1536]{3,2,1,0:T(8,128)(2,1)}), bf16[8,5,512,1536]{3,2,1,0:T(8,128)(2,1)}, u32[]{:S(2)}, u32[]{:S(2)}) %all-to-all-start.3) | async-done | bytes 62914592 | tf_op jit(solution)/shard_map/all_to_all | solution.py:76
  2984.1 349.7 %gather_fusion = bf16[16384,1536]{1,0:T(8,128)(2,1)} fusion(bf16[20480,1536]{1,0:T(8,128)(2,1)} %bitcast.17, s32[16384]{0:T(1024)S(1)} %broadcast_clamp_fusion), kind=kCustom, calls=%fused_computation.2 | custom fusion | bytes 100728832 | tf_op jit(solution)/shard_map/jit(_take)/gather | solution.py:28
  3333.7 128.9 %fusion.7 = bf16[2048,1536]{1,0:T(8,128)(2,1)} fusion(bf16[16384,1536]{1,0:T(8,128)(2,1)} %gather_fusion, pred[2048,8]{1,0:T(8,128)(4,1)S(1)} %get-tuple-element.22), kind=kLoop, calls=%fused_computation.19 | loop fusion | flops 47185920 | bytes 56639488 | tf_op jit(solution)/shard_map/reduce_sum | solution.py:79
  (25 shorter events, 0.1 us)
Async XLA Ops:
  8.3 270.0 %copy-start = (s32[2048,8]{1,0:T(8,128)}, s32[2048,8]{1,0:T(8,128)S(1)}, u32[]{:S(2)}) copy-start(s32[2048,8]{1,0:T(8,128)S(1)} %copy.46) | copy-start | bytes 196612
  12.1 1.5 copy-start.2
  24.6 0.6 copy-start.3
  25.4 252.9 %copy-start.5 = (s32[16384,1]{0,1:T(1,128)}, s32[16384,1]{0,1:T(1,128)S(1)}, u32[]{:S(2)}) copy-start(s32[16384,1]{0,1:T(1,128)S(1)} %compare_select_fusion.1) | copy-start | bytes 196612
  86.4 399.1 %all-to-all-start = ((f32[8,5,512]{2,1,0:T(8,128)}), f32[8,5,512]{2,1,0:T(8,128)}, u32[]{:S(2)}, u32[]{:S(2)}) async-start(f32[8,5,512]{2,1,0:T(8,128)} %reshape.105), calls=%async_computation | async-start | bytes 262144 | tf_op jit(solution)/shard_map/all_to_all | solution.py:71
  278.3 125.0 %copy-start.7 = (pred[20480]{0:T(1024)(128)(4,1)S(1)}, pred[20480]{0:T(1024)(128)(4,1)}, u32[]{:S(2)}) copy-start(pred[20480]{0:T(1024)(128)(4,1)} %compare_and_fusion.1) | copy-start | bytes 61444
  1180.9 688.3 %all-to-all-start.1 = ((bf16[8,5,512,1536]{3,2,1,0:T(8,128)(2,1)}), bf16[8,5,512,1536]{3,2,1,0:T(8,128)(2,1)}, u32[]{:S(2)}, u32[]{:S(2)}) async-start(bf16[8,5,512,1536]{3,2,1,0:T(8,128)(2,1)} %bitcast.108), calls=%async_computation.1 | async-start | bytes 125829120 | tf_op jit(solution)/shard_map/all_to_all | solution.py:70
  1190.4 101.3 %all-gather.8.cloned.1.call-start = ((), (), s32[]{:S(2)}) async-start(), calls=%async_computation.10 | async-start | bytes 11796480 | tf_op jit(solution)/shard_map/all_gather | solution.py:72
  1191.1 199.3 %all-gather.4.cloned.1.call-start = ((), (), s32[]{:S(2)}) async-start(), calls=%async_computation.8 | async-start | bytes 11796480 | tf_op jit(solution)/shard_map/all_gather | solution.py:74
  1191.8 723.2 %all-gather.6.cloned.1.call-start = ((), (), s32[]{:S(2)}) async-start(), calls=%async_computation.9 | async-start | bytes 11796480 | tf_op jit(solution)/shard_map/all_gather | solution.py:73
  1192.6 2270.1 %reduce-scatter.6.cloned.1.call-start = ((), (), s32[]{:S(2)}) async-start(), calls=%async_computation.12 | async-start | bytes 23592960 | tf_op jit(solution)/shard_map/reduce_scatter | solution.py:83
  2079.1 216.7 %all-to-all-start.4 = ((f32[8,5,512]{2,1,0:T(8,128)}), f32[8,5,512]{2,1,0:T(8,128)}, u32[]{:S(2)}, u32[]{:S(2)}) async-start(f32[8,5,512]{2,1,0:T(8,128)} %copy.57), calls=%async_computation.4 | async-start | bytes 262144 | tf_op jit(solution)/shard_map/all_to_all | solution.py:77
  2083.1 1379.6 %reduce-scatter.8.cloned.1.call-start = ((), (), s32[]{:S(2)}) async-start(), calls=%async_computation.13 | async-start | bytes 23592960 | tf_op jit(solution)/shard_map/reduce_scatter | solution.py:82
  2295.8 688.3 %all-to-all-start.3 = ((bf16[8,5,512,1536]{3,2,1,0:T(8,128)(2,1)}), bf16[8,5,512,1536]{3,2,1,0:T(8,128)(2,1)}, u32[]{:S(2)}, u32[]{:S(2)}) async-start(bf16[8,5,512,1536]{3,2,1,0:T(8,128)(2,1)} %copy.56), calls=%async_computation.3 | async-start | bytes 125829120 | tf_op jit(solution)/shard_map/all_to_all | solution.py:76
  2305.3 44.5 %copy-start.4 = (s32[16384]{0:T(1024)S(1)}, s32[16384]{0:T(1024)}, u32[]{:S(2)}) copy-start(s32[16384]{0:T(1024)} %copy-done.3) | copy-start | bytes 196612
  2305.3 45.1 %copy-start.6 = (s32[16384,1]{0,1:T(1,128)S(1)}, s32[16384,1]{0,1:T(1,128)}, u32[]{:S(2)}) copy-start(s32[16384,1]{0,1:T(1,128)} %copy-done.5) | copy-start | bytes 196612
  2305.3 1157.4 %reduce-scatter.4.cloned.1.call-start = ((), (), s32[]{:S(2)}) async-start(), calls=%async_computation.11 | async-start | bytes 23592960 | tf_op jit(solution)/shard_map/reduce_scatter | solution.py:81
  2349.7 92.7 %copy-start.1 = (s32[2048,8]{1,0:T(8,128)S(1)}, s32[2048,8]{1,0:T(8,128)}, u32[]{:S(2)}) copy-start(s32[2048,8]{1,0:T(8,128)} %copy-done) | copy-start | bytes 196612
Sparse Core Ops, SparseCore 0:
  1192.7 98.9 all-gather.7
  1293.2 97.1 all-gather.3
  1391.9 97.1 all-gather.5
  2037.3 176.4 reduce-scatter.5
  2216.5 176.4 reduce-scatter.7
  2395.7 176.4 reduce-scatter.3
where the time goes:
time: 3480 us; the launch traced here: 3470 us
  waiting for transfers between devices  1170 us (34%)
  local copies, waits for them, and re-layouts  870 us (25%)
  blocking collectives  695 us (20%)
  matrix products  469 us (13%)
  other arithmetic  221 us (6%)
    all_to_all x1, blocking collectives, per_device(): x_rows = lax.all_to_all(x_send, 'ep', 0, 0, tiled=True)  695 us
    gather x5, local copies, waits for them, and re-layouts, take_rows(): return jnp.take(rows, row_index, axis=0, mode='fill', fill_value=0)  691 us
    all_to_all x1, waiting for transfers between devices, per_device(): lax.all_to_all(dx_rows, 'ep', 0, 0, tiled=True).reshape(places, hidden)  538 us
    all_to_all x1, waiting for transfers between devices, per_device(): dy_rows = lax.all_to_all(dy_send, 'ep', 0, 0, tiled=True)  479 us
    reduce_sum x1, other arithmetic, per_device(): in_grad = jnp.sum(dx_pick, axis=1, dtype=jnp.float32).astype(jnp.bfloat16)  129 us
    all_gather x1, waiting for transfers between devices, per_device(): w_one_full = lax.all_gather(w_one, 'fsdp', axis=1, tiled=True)  97.5 us
    select_n x3, other arithmetic, take_rows(): return jnp.take(rows, row_index, axis=0, mode='fill', fill_value=0)  83.7 us
    dot_general x1, matrix products, expert_grads(): jnp.einsum('pecd,edf->pecf', x_rows, w_three, preferred_element_type=jnp....  79.3 us
  transfers between devices with their start and end apart: 10, of which 4 were waited for; matrix products, arithmetic and copies ran while one was open for 39% of the time, Pallas kernels for 0%

commit v1 on v0

v1 whole, which is shorter than its diff:
```python
import functools

import jax
import jax.numpy as jnp
from jax import lax
from jax.experimental import pallas as pl
from jax.experimental.pallas import tpu as pltpu
from jax.sharding import PartitionSpec as P

F32, BF16, I32 = jnp.float32, jnp.bfloat16, jnp.int32
COL_CHUNKS = 2
TOKENS = 256
IN_WINDOW = 96
OUT_WINDOW = 128
ALIGN = 16


def capacity_of(tok_dev, top_k, experts):
    return max(8, ((tok_dev * top_k * 5) // (4 * experts) + 7) // 8 * 8)


def route(ids_all, gates_all, first_expert, local_experts, capacity):
    ids_t = jnp.swapaxes(ids_all, 1, 2)
    gates_t = jnp.swapaxes(gates_all, 1, 2)
    mine = first_expert + jnp.arange(local_experts, dtype=I32)
    match = ids_t[:, None] == mine[None, :, None, None]
    hit = jnp.any(match, axis=2).astype(I32)
    gate_te = jnp.sum(jnp.where(match, gates_t[:, None], 0.0), axis=2)
    upto = jnp.cumsum(hit, axis=-1)
    place = jnp.where((hit > 0) & (upto <= capacity), upto - 1, -1)
    ends = jnp.minimum(upto[:, :, TOKENS - 1 :: TOKENS], capacity)
    starts = jnp.concatenate([jnp.zeros_like(ends[:, :, :1]), ends[:, :, :-1]], axis=-1)
    starts = starts // ALIGN * ALIGN
    return place, gate_te, jnp.swapaxes(starts, 1, 2), jnp.swapaxes(ends, 1, 2)


def rounds_of(starts, ends, window):
    return jnp.max((ends - starts + window - 1) // window, axis=-1)


def gather_kernel(local_experts, capacity, cols, with_gate, starts, rounds, place_ref, gate_ref, x_ref, *outs):
    src, blk = pl.program_id(0), pl.program_id(1)
    blocks = pl.num_programs(1)
    step = src * blocks + blk
    hidden = x_ref.shape[-1]
    W = IN_WINDOW

    @pl.when(blk == 0)
    def _():
        for out in outs:
            for e in range(local_experts):
                out[0, e] = jnp.zeros(out.shape[2:], out.dtype)

    def one_round(r, carry):
        picks, gates, bases = [], [], []
        for e in range(local_experts):
            low = starts[step * local_experts + e] + r * W
            base = pl.multiple_of(jnp.minimum(low, capacity - W), ALIGN)
            slot = base + lax.broadcasted_iota(I32, (W, TOKENS), 0)
            hit = (place_ref[0, e:e + 1, :] == slot) & (slot >= low)
            picks.append(jnp.where(hit, 1.0, 0.0).astype(BF16))
            if with_gate:
                gates.append(jnp.sum(jnp.where(hit, gate_ref[0, e:e + 1, :], 0.0), axis=1, keepdims=True))
            bases.append(base)
        pick = jnp.concatenate(picks, axis=0)
        for c in range(0, hidden, cols):
            rows = jnp.dot(pick, x_ref[:, c:c + cols], preferred_element_type=F32)
            for e in range(local_experts):
                part = rows[e * W:(e + 1) * W]
                at = (0, e, pl.ds(bases[e], W), slice(c, c + cols))
                outs[0][at] = outs[0][at] + part.astype(BF16)
                if with_gate:
                    outs[1][at] = outs[1][at] + (gates[e] * part).astype(BF16)
        return carry

    lax.fori_loop(0, rounds[step], one_round, 0)


def gather_rows(x_all, place8, gate8, starts, ends, local_experts, capacity, with_gate):
    sources, _, tok_dev = place8.shape
    hidden = x_all.shape[-1]
    blocks = tok_dev // TOKENS
    rounds = rounds_of(starts, ends, IN_WINDOW).reshape(-1)
    shape = jax.ShapeDtypeStruct((sources, local_experts, capacity, hidden), BF16)
    out_spec = pl.BlockSpec((1, local_experts, capacity, hidden), lambda s, b, *_: (s, 0, 0, 0))
    row_spec = pl.BlockSpec((1, 8, TOKENS), lambda s, b, *_: (s, 0, b))
    n_out = 2 if with_gate else 1
    places = sources * local_experts * capacity
    out = pl.pallas_call(
        functools.partial(gather_kernel, local_experts, capacity, 512 if hidden % 512 == 0 else hidden, with_gate),
        grid_spec=pltpu.PrefetchScalarGridSpec(
            num_scalar_prefetch=2,
            grid=(sources, blocks),
            in_specs=[row_spec, row_spec, pl.BlockSpec((TOKENS, hidden), lambda s, b, *_: (s * blocks + b, 0))],
            out_specs=[out_spec] * n_out,
        ),
        out_shape=[shape] * n_out,
        cost_estimate=pl.CostEstimate(flops=2 * places * 512 * hidden, bytes_accessed=2 * hidden * (sources * tok_dev + n_out * places), transcendentals=0),
        compiler_params=pltpu.CompilerParams(dimension_semantics=("arbitrary", "arbitrary"), vmem_limit_bytes=56 << 20),
        name="gather_rows",
    )(starts.reshape(-1), rounds, place8, gate8, x_all)
    return out


def nt_dot(a, b):
    return lax.dot_general(a, b, (((1,), (1,)), ((), ())), preferred_element_type=F32)


def combine_kernel(local_experts, capacity, starts, rounds, place_ref, dh1_ref, dh3_ref, w1_ref, w3_ref, out_ref, dx_ref):
    src = pl.program_id(0)
    blocks = out_ref.shape[1] // TOKENS
    W = OUT_WINDOW
    tile = 256 if capacity % 256 == 0 else capacity
    tiles = capacity // tile

    def one_tile(i, carry):
        e, m = i // tiles, i % tiles
        rows = pl.ds(pl.multiple_of(m * tile, tile), tile)
        dx = nt_dot(dh1_ref[0, e, rows, :], w1_ref[e]) + nt_dot(dh3_ref[0, e, rows, :], w3_ref[e])
        dx_ref[e, rows, :] = dx.astype(BF16)
        return carry

    lax.fori_loop(0, local_experts * tiles, one_tile, 0)

    def one_block(b, carry):
        step = src * blocks + b
        toks = pl.ds(pl.multiple_of(b * TOKENS, TOKENS), TOKENS)
        place = place_ref[0, toks, :]

        def part(r):
            picks, rows = [], []
            for e in range(local_experts):
                low = starts[step * local_experts + e] + r * W
                base = pl.multiple_of(jnp.minimum(low, capacity - W), ALIGN)
                slot = base + lax.broadcasted_iota(I32, (TOKENS, W), 1)
                hit = (place[:, e:e + 1] == slot) & (slot >= low)
                picks.append(jnp.where(hit, 1.0, 0.0).astype(BF16))
                rows.append(dx_ref[e, pl.ds(base, W), :])
            return jnp.dot(jnp.concatenate(picks, axis=1), jnp.concatenate(rows, axis=0), preferred_element_type=F32)

        out_ref[0, toks, :] = part(0)

        def more(r, c):
            out_ref[0, toks, :] += part(r)
            return c

        lax.fori_loop(1, rounds[step], more, 0)
        return carry

    lax.fori_loop(0, blocks, one_block, 0)


def combine_rows(dh1, dh3, w1, w3, place_t, starts, ends, chunk, cols):
    sources, local_experts, capacity, ff = dh1.shape
    tok_dev = place_t.shape[1]
    rounds = rounds_of(starts, ends, OUT_WINDOW).reshape(-1)
    dh_spec = pl.BlockSpec((1, local_experts, capacity, ff), lambda s, *_: (s, 0, 0, 0))
    w_spec = pl.BlockSpec((local_experts, cols, ff), lambda s, *_: (0, chunk, 0))
    places = sources * local_experts * capacity
    return pl.pallas_call(
        functools.partial(combine_kernel, local_experts, capacity),
        grid_spec=pltpu.PrefetchScalarGridSpec(
            num_scalar_prefetch=2,
            grid=(sources,),
            in_specs=[pl.BlockSpec((1, tok_dev, 8), lambda s, *_: (s, 0, 0)), dh_spec, dh_spec, w_spec, w_spec],
            out_specs=pl.BlockSpec((1, tok_dev, cols), lambda s, *_: (s, 0, 0)),
            scratch_shapes=[pltpu.VMEM((local_experts, capacity, cols), BF16)],
        ),
        out_shape=jax.ShapeDtypeStruct((sources, tok_dev, cols), F32),
        cost_estimate=pl.CostEstimate(flops=2 * places * cols * (2 * ff + 512), bytes_accessed=4 * sources * tok_dev * cols + 4 * places * ff, transcendentals=0),
        compiler_params=pltpu.CompilerParams(dimension_semantics=("arbitrary",), vmem_limit_bytes=58 << 20),
        name="combine_rows",
    )(starts.reshape(-1), rounds, place_t, dh1, dh3, w1, w3)


def fsdp_full(part, other, pos, axis):
    size = part.shape[axis]
    shape = part.shape[:axis] + (2 * size,) + part.shape[axis + 1:]
    full = lax.dynamic_update_slice_in_dim(jnp.zeros(shape, part.dtype), part, pos * size, axis)
    return lax.dynamic_update_slice_in_dim(full, other, (1 - pos) * size, axis)


def dot(spec, a, b):
    return jnp.einsum(spec, a, b, preferred_element_type=F32)


def solution(mesh):
    ep_size = mesh.shape["ep"]
    tok_spec = P(("fsdp", "ep"), None)
    up_spec = P("ep", "fsdp", None)
    down_spec = P("ep", None, "fsdp")
    swap = [(0, 1), (1, 0)]

    def per_device(layer_in, out_grad, expert_ids, gate_vals, w_one, w_two, w_three):
        tok_dev, hidden = layer_in.shape
        top_k = expert_ids.shape[1]
        local_experts = w_one.shape[0]
        experts = local_experts * ep_size
        capacity = capacity_of(tok_dev, top_k, experts)
        fpos = lax.axis_index("fsdp")
        epos = lax.axis_index("ep")
        ids_all = lax.all_gather(expert_ids, "ep")
        gates_all = lax.all_gather(gate_vals, "ep")
        x_all = lax.all_gather(layer_in, "ep", tiled=True)
        u_all = lax.all_gather(out_grad, "ep", tiled=True)
        w1 = fsdp_full(w_one, lax.ppermute(w_one, "fsdp", swap), fpos, 1)
        w3 = fsdp_full(w_three, lax.ppermute(w_three, "fsdp", swap), fpos, 1)
        w2 = fsdp_full(w_two, lax.ppermute(w_two, "fsdp", swap), fpos, 2)
        place, gate_te, starts, ends = route(ids_all, gates_all, epos * local_experts, local_experts, capacity)
        pad = ((0, 0), (0, 8 - local_experts), (0, 0))
        place8 = jnp.pad(place, pad, constant_values=-1)
        gate8 = jnp.pad(gate_te, pad)
        place_t = jnp.swapaxes(place8, 1, 2)

        def over_fsdp(grad, axis):
            size = grad.shape[axis] // 2
            away = lax.dynamic_slice_in_dim(grad, (1 - fpos) * size, size, axis)
            keep = lax.dynamic_slice_in_dim(grad, fpos * size, size, axis)
            return keep, lax.ppermute(away, "fsdp", swap)

        x_rows, = gather_rows(x_all, place8, gate8, starts, ends, local_experts, capacity, False)
        h1 = dot("pecd,edf->pecf", x_rows, w1)
        h3 = dot("pecd,edf->pecf", x_rows, w3)
        sig = jax.nn.sigmoid(h1)
        silu = h1 * sig
        act = (silu * h3).astype(BF16)
        u_rows, g_rows = gather_rows(u_all, place8, gate8, starts, ends, local_experts, capacity, True)
        grad2 = dot("pecf,pecd->efd", act, g_rows)
        g_rows, grad2 = lax.optimization_barrier((g_rows, grad2))
        keep2, other2 = over_fsdp(grad2, 2)
        da = dot("pecd,efd->pecf", g_rows, w2)
        dh1 = (da * h3 * sig * (1.0 + h1 * (1.0 - sig))).astype(BF16)
        dh3 = (da * silu).astype(BF16)

        cols = hidden // COL_CHUNKS
        dx_parts = []
        for c in range(COL_CHUNKS):
            part = combine_rows(dh1, dh3, w1, w3, place_t, starts, ends, c, cols)
            dx_parts.append(lax.psum_scatter(part, "ep", scatter_dimension=0, tiled=True)[0].astype(BF16))
        in_grad = jnp.concatenate(dx_parts, axis=-1)

        grad1 = dot("pecd,pecf->edf", x_rows, dh1)
        keep1, other1 = over_fsdp(grad1, 1)
        grad3 = dot("pecd,pecf->edf", x_rows, dh3)
        keep3, other3 = over_fsdp(grad3, 1)

        v = dot("pecd,efd->pecf", u_rows, w2)
        slot_dgate = jnp.sum(act.astype(F32) * v, axis=-1)
        spots = jnp.arange(capacity, dtype=I32)
        dense = jnp.sum(jnp.where(place[..., None] == spots, slot_dgate[:, :, None, :], 0.0), axis=-1)
        back = lax.all_to_all(dense, "ep", 0, 0, tiled=True).reshape(experts, tok_dev)
        every = jnp.arange(experts, dtype=I32)[:, None, None]
        gate_out = jnp.sum(jnp.where(expert_ids[None] == every, back[..., None], 0.0), axis=0)
        return in_grad, gate_out, keep1 + other1, keep2 + other2, keep3 + other3

    return jax.shard_map(per_device, mesh=mesh, in_specs=(tok_spec, tok_spec, tok_spec, tok_spec, up_spec, down_spec, up_spec), out_specs=(tok_spec, tok_spec, up_spec, down_spec, up_spec), check_vma=False)
```

time: 3480 us -> 1440 us (0.41)
  local copies, waits for them, and re-layouts: 870 us -> 86.4 us
  waiting for transfers between devices: 1170 us -> 443 us
  blocking collectives: 695 us -> 44.6 us
  Pallas kernels: 0 us -> 373 us
  other arithmetic: 221 us -> 100 us
  matrix products: 469 us -> 356 us
    all_to_all x4 -> x0, waiting for transfers between devices: 1020 us -> none  [the longest x1 538 us: per_device(): lax.all_to_all(dx_rows, 'ep', 0, 0, tiled=True).reshape(places, hidden)]
    gather x5 -> x0, local copies, waits for them, and re-layouts: 691 us -> none  [take_rows(): return jnp.take(rows, row_index, axis=0, mode='fill', fill_value=0)]
    all_to_all x1, blocking collectives: 695 us -> 21.9 us  [per_device(): lax.all_to_all(dense, 'ep', 0, 0, tiled=True).reshape(experts, tok_dev)]
    ppermute x0 -> x6, waiting for transfers between devices: none -> 427 us  [the longest x3 284 us: over_fsdp(): return (keep, lax.ppermute(away, 'fsdp', swap))]
    pallas_call x0 -> x4, Pallas kernels: none -> 373 us  [the longest x2 201 us: combine_rows(): pl.pallas_call(functools.partial(combine_kernel, local_experts, capacity)...]
    all_gather x3 -> x2, waiting for transfers between devices: 151 us -> 14.3 us  [the longest x1 14.3 us: per_device(): u_all = lax.all_gather(out_grad, 'ep', tiled=True)]
    scatter x2 -> x0, local copies, waits for them, and re-layouts: 121 us -> none  [the longest x1 60.7 us: slot_sources(): jnp.full((places,), tok_dev, jnp.int32).at[slot_of]]
    dot_general x9 -> x7, matrix products: 469 us -> 356 us  [dot(): return jnp.einsum(spec, a, b, preferred_element_type=F32)]
  transfers between devices with their start and end apart: 10 -> 10, of which waited for: 4 -> 5; matrix products, arithmetic and copies ran while one was open for 39% -> 30% of each run, Pallas kernels for 0% -> 12%
where the time goes in v1:
time: 1440 us; the launch traced here: 1430 us
  waiting for transfers between devices  443 us (31%)
  Pallas kernels  373 us (26%)
  matrix products  356 us (25%)
  other arithmetic  100 us (7%)
  local copies, waits for them, and re-layouts  86.4 us (6%)
  blocking collectives  44.6 us (3%)
    dot_general x7, matrix products, dot(): return jnp.einsum(spec, a, b, preferred_element_type=F32)  356 us
    ppermute x3, waiting for transfers between devices, over_fsdp(): return (keep, lax.ppermute(away, 'fsdp', swap))  284 us
    pallas_call x2, Pallas kernels, combine_rows(): pl.pallas_call(functools.partial(combine_kernel, local_experts, capacity)...  201 us
    pallas_call x2, Pallas kernels, gather_rows(): pl.pallas_call(functools.partial(gather_kernel, local_experts, capacity,...  172 us
    ppermute x1, waiting for transfers between devices, per_device(): w2 = fsdp_full(w_two, lax.ppermute(w_two, 'fsdp', swap), fpos, 2)  79 us
    ppermute x1, waiting for transfers between devices, per_device(): w3 = fsdp_full(w_three, lax.ppermute(w_three, 'fsdp', swap), fpos, 1)  64.2 us
    reduce_sum x1, other arithmetic, per_device(): jnp.sum(jnp.where(place[..., None] == spots, slot_dgate[:, :, None, :], 0...  32.4 us
    add x3, other arithmetic, per_device(): return (in_grad, gate_out, keep1 + other1, keep2 + other2, keep3 + other3)  31 us
  transfers between devices with their start and end apart: 10, of which 5 were waited for; matrix products, arithmetic and copies ran while one was open for 30% of the time, Pallas kernels for 12%

profile of v1, /device:TPU:0, one launch (start us, length us, event | category | flops | bytes accessed | tf_op | source)
XLA Modules:
  0.0 1427.2 jit_solution(5249002908777930053)
XLA Ops:
  7.2 0.7 all-gather.7.cloned.1.call-update
  8.0 0.7 all-gather.5.cloned.1.call-update
  8.7 3.3 collective-permute-start.1
  12.1 2.0 collective-permute-start
  14.1 9.8 all-gather
  23.9 1.0 compare_reduce_fusion
  24.9 3.4 copy.60
  28.4 3.8 convert_element_type.50
  32.2 5.2 copy.61
  37.4 11.3 reduce-window.6
  49.2 0.9 reduce-window.9
  50.2 4.6 copy.64
  54.8 3.1 slice.14
  58.0 0.7 reshape.64.starts
  59.1 0.6 reshape.66.rounds
  59.7 0.6 reshape.65.rounds
  60.3 8.2 add_select_fusion
  68.5 5.2 copy.94
  73.8 12.9 all-gather.1
  86.7 0.8 fusion.17
  87.5 0.9 pad.10.gate_ref
  88.4 0.8 pad.9.clone.place_ref
  89.2 3.9 broadcast.78.clone
  93.1 2.3 constant_dynamic-update-slice_fusion.3
  95.4 3.9 broadcast.78.clone.1
  99.3 2.3 constant_dynamic-update-slice_fusion.1
  101.5 4.3 broadcast_in_dim.52
  105.9 2.3 constant_dynamic-update-slice_fusion.5
  108.1 1.5 slice-done.1
  109.6 3.9 pad_bitcast_fusion.place_ref
  113.5 4.5 constant_dynamic-update-slice_fusion.2.w1_ref
  117.9 64.2 %collective-permute-done.2 = bf16[5,768,512]{2,1,0:T(8,128)(2,1)} collective-permute-done((bf16[5,768,512]{2,1,0:T(8,128)(2,1)}, bf16[5,768,512]{2,1,0:T(8,128)(2,1)}, u32[]{:S(2)}, u32[]{:S(2)}) %collective-permute-start.2) | collective-permute-done | bytes 3932192 | tf_op jit(solution)/shard_map/ppermute | solution.py:207
  182.1 4.5 constant_dynamic-update-slice_fusion.w3_ref
  186.6 79.0 %collective-permute-done = bf16[5,512,768]{2,1,0:T(8,128)(2,1)} collective-permute-done((bf16[5,512,768]{2,1,0:T(8,128)(2,1)}, bf16[5,512,768]{2,1,0:T(8,128)(2,1)}, u32[]{:S(2)}, u32[]{:S(2)}) %collective-permute-start) | collective-permute-done | bytes 3932192 | tf_op jit(solution)/shard_map/ppermute | solution.py:208
  265.5 4.3 constant_dynamic-update-slice_fusion.4
  269.8 76.3 %gather_rows.3 = bf16[8,5,512,1536]{3,2,1,0:T(8,128)(2,1)} custom-call(s32[320]{0:T(512)} %reshape.64.starts, s32[64]{0:T(128)} %reshape.66.rounds, s32[8,8,2048]{2,1,0:T(8,128)} %pad.9.clone.place_ref, f32[8,8,2048]{2,1,0:T(8,128)} %pad.10.gate_ref, bf16[16384,1536]{1,0:T(8,128)(2,1)} %all-gather.7.cloned.1.call-done.x_ref), custom_call_target="tpu_custom_call" | custom-call | flops 32212254720 | bytes 113246208 | tf_op jit(solution)/shard_map/gather_rows/pallas_call | solution.py:89
  346.2 46.0 %fusion.12 = f32[5,512,8,512]{1,3,0,2:T(8,128)} fusion(bf16[8,5,512,1536]{3,2,1,0:T(8,128)(2,1)} %gather_rows.3, bf16[5,1536,512]{2,1,0:T(8,128)(2,1)} %constant_dynamic-update-slice_fusion.2.w1_ref), kind=kOutput, calls=%fused_computation.22 | convolution fusion | flops 32212254720 | bytes 112721920 | tf_op jit(solution)/shard_map/pecd,edf->pecf/dot_general | solution.py:184
  392.1 67.1 %fusion.5 = (bf16[8,5,512,512]{3,2,1,0:T(8,128)(2,1)}, f32[5,512,8,512]{1,3,0,2:T(8,128)}) fusion(f32[5,512,8,512]{1,3,0,2:T(8,128)} %fusion.12, bf16[8,5,512,1536]{3,2,1,0:T(8,128)(2,1)} %gather_rows.3, bf16[5,1536,512]{2,1,0:T(8,128)(2,1)} %constant_dynamic-update-slice_fusion.w3_ref), kind=kOutput, calls=%fused_computation.11 | convolution fusion | flops 32275169280 | bytes 175636480 | tf_op jit(solution)/shard_map/pecd,edf->pecf/dot_general | solution.py:184
  459.3 14.3 %all-gather.5.cloned.1.call-done.x_ref = bf16[16384,1536]{1,0:T(8,128)(2,1)} async-done(((bf16[2048,1536]{1,0:T(8,128)(2,1)}), bf16[16384,1536]{1,0:T(8,128)(2,1)}) %all-gather.5.cloned.1.call-update) | async-done | bytes 50331664 | tf_op jit(solution)/shard_map/all_gather | solution.py:205
  473.6 96.1 %gather_rows.2 = (bf16[8,5,512,1536]{3,2,1,0:T(8,128)(2,1)}, bf16[8,5,512,1536]{3,2,1,0:T(8,128)(2,1)}) custom-call(s32[320]{0:T(512)} %reshape.64.starts, s32[64]{0:T(128)} %reshape.66.rounds, s32[8,8,2048]{2,1,0:T(8,128)} %pad.9.clone.place_ref, f32[8,8,2048]{2,1,0:T(8,128)} %pad.10.gate_ref, bf16[16384,1536]{1,0:T(8,128)(2,1)} %all-gather.5.cloned.1.call-done.x_ref), custom_call_target="tpu_custom_call" | custom-call | flops 32212254720 | bytes 176160768 | tf_op jit(solution)/shard_map/gather_rows/pallas_call | solution.py:89
  569.6 42.1 %convolution_bitcast_fusion.2 = f32[5,512,1536]{2,1,0:T(8,128)} fusion(bf16[8,5,512,512]{3,2,1,0:T(8,128)(2,1)} %get-tuple-element.17, bf16[8,5,512,1536]{3,2,1,0:T(8,128)(2,1)} %get-tuple-element.10), kind=kOutput, calls=%fused_computation.32 | convolution fusion | flops 32212254720 | bytes 99614720 | tf_op jit(solution)/shard_map/pecf,pecd->efd/dot_general | solution.py:184
  611.7 72.2 %fusion.4 = (bf16[8,5,512,512]{3,2,1,0:T(8,128)(2,1)}, bf16[8,5,512,512]{3,2,1,0:T(8,128)(2,1)}) fusion(f32[5,512,8,512]{1,3,0,2:T(8,128)} %fusion.12, f32[5,512,8,512]{1,3,0,2:T(8,128)} %get-tuple-element.18, bf16[8,5,512,1536]{3,2,1,0:T(8,128)(2,1)} %get-tuple-element.10, bf16[5,512,1536]{2,1,0:T(8,128)(2,1)} %constant_dynamic-update-slice_fusion.4), kind=kOutput, calls=%fused_computation.9 | convolution fusion | flops 32348569600 | bytes 196608000 | tf_op jit(solution)/shard_map/pecd,efd->pecf/dot_general | solution.py:184
  683.9 100.2 %combine_rows.2 = f32[8,2048,768]{2,1,0:T(8,128)} custom-call(s32[320]{0:T(512)} %reshape.64.starts, s32[64]{0:T(128)} %reshape.65.rounds, s32[8,2048,8]{2,1,0:T(8,128)} %pad_bitcast_fusion.place_ref, bf16[8,5,512,512]{3,2,1,0:T(8,128)(2,1)} %get-tuple-element.16.dh1_ref, bf16[8,5,512,512]{3,2,1,0:T(8,128)(2,1)} %get-tuple-element.15.dh3_ref, ...), custom_call_target="tpu_custom_call" | custom-call | flops 48318382080 | bytes 92274688 | tf_op jit(solution)/shard_map/combine_rows/pallas_call | solution.py:160
  784.2 100.4 %combine_rows.3 = f32[8,2048,768]{2,1,0:T(8,128)} custom-call(s32[320]{0:T(512)} %reshape.64.starts, s32[64]{0:T(128)} %reshape.65.rounds, s32[8,2048,8]{2,1,0:T(8,128)} %pad_bitcast_fusion.place_ref, bf16[8,5,512,512]{3,2,1,0:T(8,128)(2,1)} %get-tuple-element.16.dh1_ref, bf16[8,5,512,512]{3,2,1,0:T(8,128)(2,1)} %get-tuple-element.15.dh3_ref, ...), custom_call_target="tpu_custom_call" | custom-call | flops 48318382080 | bytes 92274688 | tf_op jit(solution)/shard_map/combine_rows/pallas_call | solution.py:160
  884.6 7.3 constant_dynamic-slice_fusion.1
  892.0 1.5 collective-permute-start.4
  893.5 43.9 %convolution_bitcast_fusion = f32[5,1536,512]{2,1,0:T(8,128)} fusion(bf16[8,5,512,1536]{3,2,1,0:T(8,128)(2,1)} %gather_rows.3, bf16[8,5,512,512]{3,2,1,0:T(8,128)(2,1)} %get-tuple-element.15.dh3_ref), kind=kOutput, calls=%fused_computation.30 | convolution fusion | flops 32212254720 | bytes 99614720 | tf_op jit(solution)/shard_map/pecd,pecf->edf/dot_general | solution.py:184
  937.4 7.9 constant_dynamic-slice_fusion
  945.3 0.5 collective-permute-start.5
  945.8 44.2 %convolution_bitcast_fusion.1 = f32[5,1536,512]{2,1,0:T(8,128)} fusion(bf16[8,5,512,1536]{3,2,1,0:T(8,128)(2,1)} %gather_rows.3, bf16[8,5,512,512]{3,2,1,0:T(8,128)(2,1)} %get-tuple-element.16.dh1_ref), kind=kOutput, calls=%fused_computation.31 | convolution fusion | flops 32212254720 | bytes 99614720 | tf_op jit(solution)/shard_map/pecd,pecf->edf/dot_general | solution.py:184
  990.0 7.9 constant_dynamic-slice_fusion.2
  997.9 1.5 collective-permute-start.3
  999.4 40.9 %fusion = f32[8,5,512]{2,1,0:T(8,128)S(1)} fusion(bf16[8,5,512,512]{3,2,1,0:T(8,128)(2,1)} %get-tuple-element.17, bf16[8,5,512,1536]{3,2,1,0:T(8,128)(2,1)} %get-tuple-element.11, bf16[5,512,1536]{2,1,0:T(8,128)(2,1)} %constant_dynamic-update-slice_fusion.4), kind=kOutput, calls=%fused_computation.3 | convolution fusion | flops 32243691520 | bytes 91832320 | tf_op jit(solution)/shard_map/pecd,efd->pecf/dot_general | solution.py:184
  1040.4 32.4 %select_reduce_fusion = f32[8,5,2048]{2,1,0:T(8,128)S(1)} fusion(f32[8,5,512]{2,1,0:T(8,128)S(1)} %fusion, s32[8,5,2048]{2,1,0:T(8,128)S(1)} %copy-done.1), kind=kLoop, calls=%fused_computation | loop fusion | flops 125747200 | bytes 737280 | tf_op jit(solution)/shard_map/reduce_sum | solution.py:250
  1072.8 21.9 %all_to_all.5 = f32[8,5,2048]{2,1,0:T(8,128)S(1)} all-to-all(f32[8,5,2048]{2,1,0:T(8,128)S(1)} %select_reduce_fusion), channel_id=1, replica_groups=mesh['fsdp'=2,'ep'=8] {'ep'}, dimensions={0} | all-to-all | bytes 655360 | tf_op jit(solution)/shard_map/all_to_all | solution.py:251
  1094.8 0.9 select_reduce_fusion.1
  1095.7 9.7 dynamic-slice_add_fusion.1
  1105.4 127.2 %collective-permute-done.5 = f32[5,768,512]{2,1,0:T(8,128)} collective-permute-done((f32[5,768,512]{2,1,0:T(8,128)}, f32[5,768,512]{2,1,0:T(8,128)}, u32[]{:S(2)}, u32[]{:S(2)}) %collective-permute-start.5) | collective-permute-done | bytes 7864352 | tf_op jit(solution)/shard_map/ppermute | solution.py:219
  1232.6 10.7 dynamic-slice_add_fusion
  1243.2 157.1 %collective-permute-done.3 = f32[5,768,512]{2,1,0:T(8,128)} collective-permute-done((f32[5,768,512]{2,1,0:T(8,128)}, f32[5,768,512]{2,1,0:T(8,128)}, u32[]{:S(2)}, u32[]{:S(2)}) %collective-permute-start.3) | collective-permute-done | bytes 7864352 | tf_op jit(solution)/shard_map/ppermute | solution.py:219
  1400.4 10.7 dynamic-slice_add_fusion.2
  1411.0 3.1 convert_bitcast_fusion.1
  1414.1 3.1 convert_bitcast_fusion
  1417.2 3.2 pad_maximum_fusion
  (41 shorter events, 1.4 us)
Async XLA Ops:
  7.2 6.9 copy-start.5
  7.2 262.7 %all-gather.7.cloned.1.call-start = ((), (), s32[]{:S(2)}) async-start(), calls=%async_computation.4 | async-start | bytes 56623104 | tf_op jit(solution)/shard_map/all_gather | solution.py:204
  7.9 465.7 %all-gather.5.cloned.1.call-start = ((), (), s32[]{:S(2)}) async-start(), calls=%async_computation.3 | async-start | bytes 56623104 | tf_op jit(solution)/shard_map/all_gather | solution.py:205
  8.7 1402.4 %reduce-scatter.3.cloned.1.call-start = ((), (), s32[]{:S(2)}) async-start(), calls=%async_computation.5 | async-start | bytes 56623104 | tf_op jit(solution)/shard_map/reduce_scatter | solution.py:239
  8.7 104.8 %collective-permute-start.1 = (bf16[5,768,512]{2,1,0:T(8,128)(2,1)}, bf16[5,768,512]{2,1,0:T(8,128)(2,1)}, u32[]{:S(2)}, u32[]{:S(2)}) collective-permute-start(bf16[5,768,512]{2,1,0:T(8,128)(2,1)} %param.11), channel_id=1, source_target_pairs={{0,8},{8,0},{1,9},{9,1},{2,10},{10,2},{3,11},{11,3},{4,12},{12,4},... | collective-permute-start | bytes 11796488 | tf_op jit(solution)/shard_map/ppermute | solution.py:206
  12.1 170.1 %collective-permute-start.2 = (bf16[5,768,512]{2,1,0:T(8,128)(2,1)}, bf16[5,768,512]{2,1,0:T(8,128)(2,1)}, u32[]{:S(2)}, u32[]{:S(2)}) collective-permute-start(bf16[5,768,512]{2,1,0:T(8,128)(2,1)} %param.13), channel_id=1, source_target_pairs={{0,8},{8,0},{1,9},{9,1},{2,10},{10,2},{3,11},{11,3},{4,12},{12,4},... | collective-permute-start | bytes 11796488 | tf_op jit(solution)/shard_map/ppermute | solution.py:207
  12.1 253.4 %collective-permute-start = (bf16[5,512,768]{2,1,0:T(8,128)(2,1)}, bf16[5,512,768]{2,1,0:T(8,128)(2,1)}, u32[]{:S(2)}, u32[]{:S(2)}) collective-permute-start(bf16[5,512,768]{2,1,0:T(8,128)(2,1)} %param.12), channel_id=1, source_target_pairs={{0,8},{8,0},{1,9},{9,1},{2,10},{10,2},{3,11},{11,3},{4,12},{12,4},... | collective-permute-start | bytes 11796488 | tf_op jit(solution)/shard_map/ppermute | solution.py:208
  68.5 5.3 copy-start.7
  73.8 21.6 %copy-start = (s32[8,5,2048]{2,1,0:T(8,128)}, s32[8,5,2048]{2,1,0:T(8,128)S(1)}, u32[]{:S(2)}) copy-start(s32[8,5,2048]{2,1,0:T(8,128)S(1)} %copy.94) | copy-start | bytes 983044
  73.8 19.3 %copy-start.2 = (bf16[5,768,512]{2,1,0:T(8,128)(2,1)S(1)}, bf16[5,768,512]{2,1,0:T(8,128)(2,1)}, u32[]{:S(2)}) copy-start(bf16[5,768,512]{2,1,0:T(8,128)(2,1)} %param.11) | copy-start | bytes 11796484
  93.1 6.2 copy-start.3
  99.3 6.6 copy-start.4
  101.5 6.6 slice-start
  105.9 3.7 slice-start.1
  784.2 630.0 %reduce-scatter.5.cloned.1.call-start = ((), (), s32[]{:S(2)}) async-start(), calls=%async_computation.6 | async-start | bytes 56623104 | tf_op jit(solution)/shard_map/reduce_scatter | solution.py:239
  892.0 203.8 %collective-permute-start.4 = (f32[5,512,768]{2,1,0:T(8,128)}, f32[5,512,768]{2,1,0:T(8,128)}, u32[]{:S(2)}, u32[]{:S(2)}) collective-permute-start(f32[5,512,768]{2,1,0:T(8,128)} %constant_dynamic-slice_fusion.1), channel_id=1, source_target_pairs={{0,8},{8,0},{1,9},{9,1},{2,10},{10,2},{3,11},{11,3},{4,12},{12,4},... | collective-permute-start | bytes 23592968 | tf_op jit(solution)/shard_map/ppermute | solution.py:219
  945.3 287.3 %collective-permute-start.5 = (f32[5,768,512]{2,1,0:T(8,128)}, f32[5,768,512]{2,1,0:T(8,128)}, u32[]{:S(2)}, u32[]{:S(2)}) collective-permute-start(f32[5,768,512]{2,1,0:T(8,128)} %constant_dynamic-slice_fusion), channel_id=1, source_target_pairs={{0,8},{8,0},{1,9},{9,1},{2,10},{10,2},{3,11},{11,3},{4,12},{12,4},... | collective-permute-start | bytes 23592968 | tf_op jit(solution)/shard_map/ppermute | solution.py:219
  997.9 402.4 %collective-permute-start.3 = (f32[5,768,512]{2,1,0:T(8,128)}, f32[5,768,512]{2,1,0:T(8,128)}, u32[]{:S(2)}, u32[]{:S(2)}) collective-permute-start(f32[5,768,512]{2,1,0:T(8,128)} %constant_dynamic-slice_fusion.2), channel_id=1, source_target_pairs={{0,8},{8,0},{1,9},{9,1},{2,10},{10,2},{3,11},{11,3},{4,12},{12,4},... | collective-permute-start | bytes 23592968 | tf_op jit(solution)/shard_map/ppermute | solution.py:219
  999.4 40.9 %copy-start.1 = (s32[8,5,2048]{2,1,0:T(8,128)S(1)}, s32[8,5,2048]{2,1,0:T(8,128)}, u32[]{:S(2)}) copy-start(s32[8,5,2048]{2,1,0:T(8,128)} %copy-done) | copy-start | bytes 983044
  999.4 95.4 %copy-start.6 = (s32[2048,8]{0,1:T(8,128)S(1)}, s32[2048,8]{0,1:T(8,128)}, u32[]{:S(2)}) copy-start(s32[2048,8]{0,1:T(8,128)} %param.9) | copy-start | bytes 196612
Sparse Core Ops, SparseCore 0:
  9.9 233.3 all-gather.6
  245.1 228.4 all-gather.4
  784.3 286.6 reduce-scatter.2
  1074.4 277.2 reduce-scatter.4

commit v2 on v1

--- a/solution.py
+++ b/solution.py
@@ -7,8 +7,8 @@
 from jax.experimental.pallas import tpu as pltpu
 from jax.sharding import PartitionSpec as P
 
+
 F32, BF16, I32 = jnp.float32, jnp.bfloat16, jnp.int32
-COL_CHUNKS = 2
 TOKENS = 256
 IN_WINDOW = 96
 OUT_WINDOW = 128
@@ -191,7 +191,7 @@
     down_spec = P("ep", None, "fsdp")
     swap = [(0, 1), (1, 0)]
 
-    def per_device(layer_in, out_grad, expert_ids, gate_vals, w_one, w_two, w_three):
+    def body(layer_in, out_grad, expert_ids, gate_vals, w_one, w_two, w_three):
         tok_dev, hidden = layer_in.shape
         top_k = expert_ids.shape[1]
         local_experts = w_one.shape[0]
@@ -199,52 +199,82 @@
         capacity = capacity_of(tok_dev, top_k, experts)
         fpos = lax.axis_index("fsdp")
         epos = lax.axis_index("ep")
+        half = hidden // 2
         ids_all = lax.all_gather(expert_ids, "ep")
         gates_all = lax.all_gather(gate_vals, "ep")
         x_all = lax.all_gather(layer_in, "ep", tiled=True)
-        u_all = lax.all_gather(out_grad, "ep", tiled=True)
-        w1 = fsdp_full(w_one, lax.ppermute(w_one, "fsdp", swap), fpos, 1)
-        w3 = fsdp_full(w_three, lax.ppermute(w_three, "fsdp", swap), fpos, 1)
-        w2 = fsdp_full(w_two, lax.ppermute(w_two, "fsdp", swap), fpos, 2)
+        w_one_other = lax.ppermute(w_one, "fsdp", swap)
+        w_three_other = lax.ppermute(w_three, "fsdp", swap)
+        w_two_other = lax.ppermute(w_two, "fsdp", swap)
+        w2a = jnp.where(fpos == 0, w_two, w_two_other)
+        w2b = jnp.where(fpos == 0, w_two_other, w_two)
         place, gate_te, starts, ends = route(ids_all, gates_all, epos * local_experts, local_experts, capacity)
         pad = ((0, 0), (0, 8 - local_experts), (0, 0))
         place8 = jnp.pad(place, pad, constant_values=-1)
         gate8 = jnp.pad(gate_te, pad)
+        low, high, x_all, w_one_other, w_three_other, place8, gate8, starts, ends = lax.optimization_barrier((out_grad[:, :half], out_grad[:, half:], x_all, w_one_other, w_three_other, place8, gate8, starts, ends))
         place_t = jnp.swapaxes(place8, 1, 2)
-
-        def over_fsdp(grad, axis):
-            size = grad.shape[axis] // 2
-            away = lax.dynamic_slice_in_dim(grad, (1 - fpos) * size, size, axis)
-            keep = lax.dynamic_slice_in_dim(grad, fpos * size, size, axis)
-            return keep, lax.ppermute(away, "fsdp", swap)
-
-        x_rows, = gather_rows(x_all, place8, gate8, starts, ends, local_experts, capacity, False)
+        w1 = fsdp_full(w_one, w_one_other, fpos, 1)
+        w3 = fsdp_full(w_three, w_three_other, fpos, 1)
+        u_all_a = lax.all_gather(low, "ep", tiled=True)
+        high, x_rows = lax.optimization_barrier((high, gather_rows(x_all, place8, gate8, starts, ends, local_experts, capacity, False)[0]))
+        u_all_b = lax.all_gather(high, "ep", tiled=True)
+
+        def pick(rows, with_gate):
+            return gather_rows(rows, place8, gate8, starts, ends, local_experts, capacity, with_gate)
+
+        def over_fsdp(low, high):
+            return jnp.where(fpos == 0, low, high), jnp.where(fpos == 0, high, low)
+
         h1 = dot("pecd,edf->pecf", x_rows, w1)
         h3 = dot("pecd,edf->pecf", x_rows, w3)
         sig = jax.nn.sigmoid(h1)
         silu = h1 * sig
         act = (silu * h3).astype(BF16)
-        u_rows, g_rows = gather_rows(u_all, place8, gate8, starts, ends, local_experts, capacity, True)
-        grad2 = dot("pecf,pecd->efd", act, g_rows)
-        g_rows, grad2 = lax.optimization_barrier((g_rows, grad2))
-        keep2, other2 = over_fsdp(grad2, 2)
-        da = dot("pecd,efd->pecf", g_rows, w2)
+        u_a, g_a = pick(u_all_a, True)
+        da_a = dot("pecd,efd->pecf", g_a, w2a)
+        u_all_b, da_a = lax.optimization_barrier((u_all_b, da_a))
+        u_b, g_b = pick(u_all_b, True)
+        da = da_a + dot("pecd,efd->pecf", g_b, w2b)
         dh1 = (da * h3 * sig * (1.0 + h1 * (1.0 - sig))).astype(BF16)
         dh3 = (da * silu).astype(BF16)
 
-        cols = hidden // COL_CHUNKS
-        dx_parts = []
-        for c in range(COL_CHUNKS):
-            part = combine_rows(dh1, dh3, w1, w3, place_t, starts, ends, c, cols)
-            dx_parts.append(lax.psum_scatter(part, "ep", scatter_dimension=0, tiled=True)[0].astype(BF16))
-        in_grad = jnp.concatenate(dx_parts, axis=-1)
-
-        grad1 = dot("pecd,pecf->edf", x_rows, dh1)
-        keep1, other1 = over_fsdp(grad1, 1)
-        grad3 = dot("pecd,pecf->edf", x_rows, dh3)
-        keep3, other3 = over_fsdp(grad3, 1)
-
-        v = dot("pecd,efd->pecf", u_rows, w2)
+        def combine(d1, d3, cols, at):
+            return combine_rows(d1, d3, w1, w3, place_t, starts, ends, at, cols)
+
+        def spread(part):
+            return lax.psum_scatter(part, "ep", scatter_dimension=0, tiled=True)[0].astype(BF16)
+
+        unit = hidden // 6
+        part0 = combine(dh1, dh3, unit, 0)
+        part0, act_l, ga_l, gb_l = lax.optimization_barrier((part0, act, g_a, g_b))
+        out0 = spread(part0)
+        keep2, away2 = over_fsdp(dot("pecf,pecd->efd", act_l, ga_l), dot("pecf,pecd->efd", act_l, gb_l))
+        away2, d1, d3 = lax.optimization_barrier((away2, dh1, dh3))
+        other2 = lax.ppermute(away2, "fsdp", swap)
+        part1 = combine(d1, d3, unit, 1)
+        part1, d1, d3 = lax.optimization_barrier((part1, d1, d3))
+        out1 = spread(part1)
+        part2 = combine(d1, d3, 2 * unit, 1)
+        part2, d1, d3, x_l = lax.optimization_barrier((part2, d1, d3, x_rows))
+        out2 = spread(part2)
+
+        def up_grad(d):
+            full = dot("pecd,pecf->edf", x_l, d)
+            return over_fsdp(full[:, :half], full[:, half:])
+
+        keep1, away1 = up_grad(d1)
+        away1, d3 = lax.optimization_barrier((away1, d3))
+        other1 = lax.ppermute(away1, "fsdp", swap)
+        keep3, away3 = up_grad(d3)
+        away3, d1, d3 = lax.optimization_barrier((away3, d1, d3))
+        other3 = lax.ppermute(away3, "fsdp", swap)
+        part3 = combine(d1, d3, 2 * unit, 2)
+        part3, u_a, u_b = lax.optimization_barrier((part3, u_a, u_b))
+        out3 = spread(part3)
+        in_grad = jnp.concatenate([out0, out1, out2, out3], axis=-1)
+
+        v = dot("pecd,efd->pecf", u_a, w2a) + dot("pecd,efd->pecf", u_b, w2b)
         slot_dgate = jnp.sum(act.astype(F32) * v, axis=-1)
         spots = jnp.arange(capacity, dtype=I32)
         dense = jnp.sum(jnp.where(place[..., None] == spots, slot_dgate[:, :, None, :], 0.0), axis=-1)
@@ -253,4 +283,4 @@
         gate_out = jnp.sum(jnp.where(expert_ids[None] == every, back[..., None], 0.0), axis=0)
         return in_grad, gate_out, keep1 + other1, keep2 + other2, keep3 + other3
 
-    return jax.shard_map(per_device, mesh=mesh, in_specs=(tok_spec, tok_spec, tok_spec, tok_spec, up_spec, down_spec, up_spec), out_specs=(tok_spec, tok_spec, up_spec, down_spec, up_spec), check_vma=False)
+    return jax.shard_map(body, mesh=mesh, in_specs=(tok_spec, tok_spec, tok_spec, tok_spec, up_spec, down_spec, up_spec), out_specs=(tok_spec, tok_spec, up_spec, down_spec, up_spec), check_vma=False)

time: 1440 us -> 1750 us (1.22)
  Pallas kernels: 373 us -> 486 us
  other arithmetic: 100 us -> 207 us
  blocking collectives: 44.6 us -> 87.9 us
  waiting for transfers between devices: 443 us -> 485 us
  matrix products: 356 us -> 389 us
  local copies, waits for them, and re-layouts: 86.4 us -> 59.6 us
    convert_element_type x2 -> x5, other arithmetic: 6.18 us -> 82.9 us  [the longest x1 73.7 us: body(): dh3 = (da * silu).astype(BF16)]
    pallas_call x2 -> x4, Pallas kernels: 201 us -> 272 us  [combine_rows(): pl.pallas_call(functools.partial(combine_kernel, local_experts, capacity)...]
    all_gather x2 -> x3, waiting for transfers between devices: 14.3 us -> 62.3 us  [the longest x1 62.3 us: body(): x_all = lax.all_gather(layer_in, 'ep', tiled=True)]
    all_to_all x1, blocking collectives: 21.9 us -> 64.8 us  [body(): lax.all_to_all(dense, 'ep', 0, 0, tiled=True).reshape(experts, tok_dev)]
    pallas_call x2 -> x3, Pallas kernels: 172 us -> 214 us  [gather_rows(): pl.pallas_call(functools.partial(gather_kernel, local_experts, capacity,...]
    dot_general x7 -> x10, matrix products: 356 us -> 389 us  [dot(): return jnp.einsum(spec, a, b, preferred_element_type=F32)]
    dynamic_slice x3 -> x0, local copies, waits for them, and re-layouts: 23.1 us -> none  [over_fsdp(): away = lax.dynamic_slice_in_dim(grad, (1 - fpos) * size, size, axis)]
    select_n x0 -> x2, other arithmetic: none -> 23.1 us  [over_fsdp(): return (jnp.where(fpos == 0, low, high), jnp.where(fpos == 0, high, low))]
  transfers between devices with their start and end apart: 10 -> 13, of which waited for: 5 -> 5; matrix products, arithmetic and copies ran while one was open for 30% -> 31% of each run, Pallas kernels for 12% -> 21%
where the time goes in v2:
time: 1750 us; the launch traced here: 1740 us
  Pallas kernels  486 us (28%)
  waiting for transfers between devices  485 us (28%)
  matrix products  389 us (22%)
  other arithmetic  207 us (12%)
  blocking collectives  87.9 us (5%)
  local copies, waits for them, and re-layouts  59.6 us (3%)
    dot_general x10, matrix products, dot(): return jnp.einsum(spec, a, b, preferred_element_type=F32)  389 us
    pallas_call x4, Pallas kernels, combine_rows(): pl.pallas_call(functools.partial(combine_kernel, local_experts, capacity)...  272 us
    pallas_call x3, Pallas kernels, gather_rows(): pl.pallas_call(functools.partial(gather_kernel, local_experts, capacity,...  214 us
    ppermute x1, waiting for transfers between devices, body(): other3 = lax.ppermute(away3, 'fsdp', swap)  173 us
    ppermute x1, waiting for transfers between devices, body(): other1 = lax.ppermute(away1, 'fsdp', swap)  154 us
    ppermute x1, waiting for transfers between devices, body(): w_three_other = lax.ppermute(w_three, 'fsdp', swap)  83.4 us
    convert_element_type x1, other arithmetic, body(): dh3 = (da * silu).astype(BF16)  73.7 us
    all_to_all x1, blocking collectives, body(): lax.all_to_all(dense, 'ep', 0, 0, tiled=True).reshape(experts, tok_dev)  64.8 us
  transfers between devices with their start and end apart: 13, of which 5 were waited for; matrix products, arithmetic and copies ran while one was open for 31% of the time, Pallas kernels for 21%

profile of v2, /device:TPU:0, one launch (start us, length us, event | category | flops | bytes accessed | tf_op | source)
XLA Modules:
  0.0 1736.4 jit_solution(1606768944089780551)
XLA Ops:
  7.9 3.3 collective-permute-start
  11.3 10.5 all-gather
  21.9 1.0 compare_reduce_fusion
  22.9 3.4 copy.74
  26.3 4.9 convert_element_type.51
  31.2 5.3 copy.75
  36.5 11.3 reduce-window.6
  48.3 0.9 reduce-window.9
  49.3 4.7 copy.78
  54.0 3.1 slice.34
  57.1 12.5 all-gather.1
  69.6 0.8 fusion.20
  70.5 0.8 pad.10.gate_ref
  71.3 5.6 add_select_fusion
  76.9 4.2 pad.9
  81.1 1.6 copy-done
  82.7 3.1 fusion.31
  85.9 11.5 collective-permute-done
  97.4 83.4 %collective-permute-done.1 = bf16[5,768,512]{2,1,0:T(8,128)(2,1)} collective-permute-done((bf16[5,768,512]{2,1,0:T(8,128)(2,1)}, bf16[5,768,512]{2,1,0:T(8,128)(2,1)}, u32[]{:S(2)}, u32[]{:S(2)}) %collective-permute-start.1) | collective-permute-done | bytes 3932192 | tf_op jit(solution)/shard_map/ppermute | solution.py:207
  180.8 62.3 %all-gather.6.cloned.1.call-done.x_ref = bf16[16384,1536]{1,0:T(8,128)(2,1)} async-done(((bf16[2048,1536]{1,0:T(8,128)(2,1)}), bf16[16384,1536]{1,0:T(8,128)(2,1)}) %all-gather.6.cloned.1.call-update) | async-done | bytes 50331664 | tf_op jit(solution)/shard_map/all_gather | solution.py:205
  243.2 0.7 reshape.72.starts
  243.9 0.9 fusion.26
  245.5 5.9 copy.79.place_ref
  251.4 77.6 %gather_rows.3 = bf16[8,5,512,1536]{3,2,1,0:T(8,128)(2,1)} custom-call(s32[320]{0:T(512)} %reshape.72.starts, s32[64]{0:T(128)} %reshape.74.rounds, s32[8,8,2048]{2,1,0:T(8,128)} %copy.79.place_ref, f32[8,8,2048]{2,1,0:T(8,128)} %pad.10.gate_ref, bf16[16384,1536]{1,0:T(8,128)(2,1)} %all-gather.6.cloned.1.call-done.x_ref), custom_call_target="tpu_custom_call" | custom-call | flops 32212254720 | bytes 113246208 | tf_op jit(solution)/shard_map/gather_rows/pallas_call | solution.py:89
  329.5 1.7 collective-permute-start.2
  331.2 4.1 broadcast.78.clone
  335.3 2.3 constant_dynamic-update-slice_fusion.1
  337.6 3.9 broadcast.78.clone.1
  341.5 2.2 constant_dynamic-update-slice_fusion.3
  343.7 7.0 constant_dynamic-update-slice_fusion
  350.7 47.3 %fusion.10 = f32[5,512,8,512]{1,3,0,2:T(8,128)} fusion(bf16[8,5,512,1536]{3,2,1,0:T(8,128)(2,1)} %gather_rows.3, bf16[5,1536,512]{2,1,0:T(8,128)(2,1)} %get-tuple-element.94.w1_ref), kind=kOutput, calls=%fused_computation.24 | convolution fusion | flops 32212254720 | bytes 112721920 | tf_op jit(solution)/shard_map/pecd,edf->pecf/dot_general | solution.py:184
  398.0 47.7 %fusion.12 = f32[5,512,8,512]{1,3,0,2:T(8,128)} fusion(bf16[8,5,512,1536]{3,2,1,0:T(8,128)(2,1)} %gather_rows.3, bf16[5,1536,512]{2,1,0:T(8,128)(2,1)} %get-tuple-element.95.w3_ref), kind=kOutput, calls=%fused_computation.26 | convolution fusion | flops 32212254720 | bytes 112721920 | tf_op jit(solution)/shard_map/pecd,edf->pecf/dot_general | solution.py:184
  446.3 68.2 %gather_rows.4 = (bf16[8,5,512,768]{3,2,1,0:T(8,128)(2,1)}, bf16[8,5,512,768]{3,2,1,0:T(8,128)(2,1)}) custom-call(s32[320]{0:T(512)} %reshape.72.starts, s32[64]{0:T(128)} %reshape.74.rounds, s32[8,8,2048]{2,1,0:T(8,128)} %copy.79.place_ref, f32[8,8,2048]{2,1,0:T(8,128)} %pad.10.gate_ref, bf16[16384,768]{1,0:T(8,128)(2,1)} %all-gather.10.cloned.1.call-done.x_ref), custom_call_target="tpu_custom_call" | custom-call | flops 16106127360 | bytes 88080384 | tf_op jit(solution)/shard_map/gather_rows/pallas_call | solution.py:89
  514.5 32.1 %convolution_bitcast_fusion = f32[8,5,512,512]{3,2,1,0:T(8,128)} fusion(bf16[8,5,512,768]{3,2,1,0:T(8,128)(2,1)} %get-tuple-element.62, bf16[5,512,768]{2,1,0:T(8,128)(2,1)} %param.12, bf16[5,512,768]{2,1,0:T(8,128)(2,1)} %collective-permute-done.2, pred[]{:T(512)S(6)} %eq.23), kind=kOutput, calls=%fused_computation.19 | convolution fusion | flops 16108093440 | bytes 81264640 | tf_op jit(solution)/shard_map/pecd,efd->pecf/dot_general | solution.py:184
  546.5 68.2 %gather_rows.5 = (bf16[8,5,512,768]{3,2,1,0:T(8,128)(2,1)}, bf16[8,5,512,768]{3,2,1,0:T(8,128)(2,1)}) custom-call(s32[320]{0:T(512)} %reshape.72.starts, s32[64]{0:T(128)} %reshape.74.rounds, s32[8,8,2048]{2,1,0:T(8,128)} %copy.79.place_ref, f32[8,8,2048]{2,1,0:T(8,128)} %pad.10.gate_ref, bf16[16384,768]{1,0:T(8,128)(2,1)} %all-gather.8.cloned.1.call-done.x_ref), custom_call_target="tpu_custom_call" | custom-call | flops 16106127360 | bytes 88080384 | tf_op jit(solution)/shard_map/gather_rows/pallas_call | solution.py:89
  614.7 32.2 %fusion.16 = f32[5,512,8,512]{1,3,0,2:T(8,128)} fusion(bf16[8,5,512,768]{3,2,1,0:T(8,128)(2,1)} %get-tuple-element.61, bf16[5,512,768]{2,1,0:T(8,128)(2,1)} %collective-permute-done.2, bf16[5,512,768]{2,1,0:T(8,128)(2,1)} %param.12, pred[]{:T(512)S(6)} %eq.23), kind=kOutput, calls=%fused_computation.37 | convolution fusion | flops 16108093440 | bytes 81264640 | tf_op jit(solution)/shard_map/pecd,efd->pecf/dot_general | solution.py:184
  647.0 73.7 %multiply_convert_fusion = (bf16[8,5,512,512]{3,2,1,0:T(8,128)(2,1)}, bf16[8,5,512,512]{3,2,1,0:T(8,128)(2,1)}, bf16[8,5,512,512]{3,2,1,0:T(8,128)(2,1)}) fusion(f32[8,5,512,512]{3,2,1,0:T(8,128)} %convolution_bitcast_fusion, f32[5,512,8,512]{1,3,0,2:T(8,128)} %fusion.16, f32[5,512,8,512]{1,3,0,2:T(8,128)} %fusion.10, f32[5,512,8,512]{1,3,0,2:T(8,128)} %fusion.12), kind=kLoop, calls=%fused_computation.18 | loop fusion | flops 167772160 | bytes 230686720 | tf_op jit(solution)/shard_map/convert_element_type | solution.py:240
  720.6 60.8 %combine_rows.4 = f32[8,2048,256]{2,1,0:T(8,128)} custom-call(s32[320]{0:T(512)} %reshape.72.starts, s32[64]{0:T(128)} %reshape.73.rounds, s32[8,2048,8]{2,1,0:T(8,128)} %bitcast.116, bf16[8,5,512,512]{3,2,1,0:T(8,128)(2,1)} %get-tuple-element.73.dh1_ref, bf16[8,5,512,512]{3,2,1,0:T(8,128)(2,1)} %get-tuple-element.74.dh3_ref, ...), custom_call_target="tpu_custom_call" | custom-call | flops 16106127360 | bytes 58720256 | tf_op jit(solution)/shard_map/combine_rows/pallas_call | solution.py:160
  781.5 26.1 %fusion.32 = f32[5,512,768,1]{2,1,0,3:T(8,128)} fusion(bf16[8,5,512,512]{3,2,1,0:T(8,128)(2,1)} %get-tuple-element.60, bf16[8,5,512,768]{3,2,1,0:T(8,128)(2,1)} %get-tuple-element.61), kind=kOutput, calls=%fused_computation.83 | convolution fusion | flops 16106127360 | bytes 60293120 | tf_op jit(solution)/shard_map/pecf,pecd->efd/dot_general | solution.py:184
  807.6 38.5 %bitcast_select_fusion.1 = (f32[5,512,768]{2,1,0:T(8,128)}, f32[5,512,768,1]{2,1,0,3:T(8,128)}) fusion(f32[5,512,768,1]{2,1,0,3:T(8,128)} %fusion.32, pred[]{:T(512)S(6)} %eq.23, bf16[8,5,512,512]{3,2,1,0:T(8,128)(2,1)} %get-tuple-element.60, bf16[8,5,512,768]{3,2,1,0:T(8,128)(2,1)} %get-tuple-element.62), kind=kOutput, calls=%fused_computation.22 | convolution fusion | flops 16108093440 | bytes 76021760 | tf_op jit(solution)/shard_map/pecf,pecd->efd/dot_general | solution.py:184
  846.1 61.1 %combine_rows.5 = f32[8,2048,256]{2,1,0:T(8,128)} custom-call(s32[320]{0:T(512)} %reshape.72.starts, s32[64]{0:T(128)} %reshape.73.rounds, s32[8,2048,8]{2,1,0:T(8,128)} %bitcast.117, bf16[8,5,512,512]{3,2,1,0:T(8,128)(2,1)} %get-tuple-element.73.dh1_ref, bf16[8,5,512,512]{3,2,1,0:T(8,128)(2,1)} %get-tuple-element.74.dh3_ref, ...), custom_call_target="tpu_custom_call" | custom-call | flops 16106127360 | bytes 58720256 | tf_op jit(solution)/shard_map/combine_rows/pallas_call | solution.py:160
  907.2 75.2 %combine_rows.6 = f32[8,2048,512]{2,1,0:T(8,128)} custom-call(s32[320]{0:T(512)} %reshape.72.starts, s32[64]{0:T(128)} %reshape.73.rounds, s32[8,2048,8]{2,1,0:T(8,128)} %bitcast.118, bf16[8,5,512,512]{3,2,1,0:T(8,128)(2,1)} %get-tuple-element.73.dh1_ref, bf16[8,5,512,512]{3,2,1,0:T(8,128)(2,1)} %get-tuple-element.74.dh3_ref, ...), custom_call_target="tpu_custom_call" | custom-call | flops 32212254720 | bytes 75497472 | tf_op jit(solution)/shard_map/combine_rows/pallas_call | solution.py:160
  982.5 45.0 %convolution_bitcast_fusion.2 = f32[5,1536,512]{2,1,0:T(8,128)} fusion(bf16[8,5,512,1536]{3,2,1,0:T(8,128)(2,1)} %gather_rows.3, bf16[8,5,512,512]{3,2,1,0:T(8,128)(2,1)} %get-tuple-element.73.dh1_ref), kind=kOutput, calls=%fused_computation.31 | convolution fusion | flops 32212254720 | bytes 99614720 | tf_op jit(solution)/shard_map/pecd,pecf->edf/dot_general | solution.py:184
  1027.5 11.2 slice_select_fusion.1
  1038.7 52.0 %convolution_bitcast_fusion.1 = f32[5,1536,512]{2,1,0:T(8,128)} fusion(bf16[8,5,512,1536]{3,2,1,0:T(8,128)(2,1)} %gather_rows.3, bf16[8,5,512,512]{3,2,1,0:T(8,128)(2,1)} %get-tuple-element.74.dh3_ref), kind=kOutput, calls=%fused_computation.30 | convolution fusion | flops 32212254720 | bytes 99614720 | tf_op jit(solution)/shard_map/pecd,pecf->edf/dot_general | solution.py:184
  1090.7 11.9 slice_select_fusion
  1102.6 75.1 %combine_rows.7 = f32[8,2048,512]{2,1,0:T(8,128)} custom-call(s32[320]{0:T(512)} %reshape.72.starts, s32[64]{0:T(128)} %reshape.73.rounds, s32[8,2048,8]{2,1,0:T(8,128)} %bitcast.119, bf16[8,5,512,512]{3,2,1,0:T(8,128)(2,1)} %get-tuple-element.73.dh1_ref, bf16[8,5,512,512]{3,2,1,0:T(8,128)(2,1)} %get-tuple-element.74.dh3_ref, ...), custom_call_target="tpu_custom_call" | custom-call | flops 32212254720 | bytes 75497472 | tf_op jit(solution)/shard_map/combine_rows/pallas_call | solution.py:160
  1177.7 5.6 copy.94
  1183.3 2.0 collective-permute-start.5
  1185.4 32.6 %fusion.14 = f32[5,512,8,512]{1,3,0,2:T(8,128)} fusion(bf16[8,5,512,768]{3,2,1,0:T(8,128)(2,1)} %get-tuple-element.79, bf16[5,512,768]{2,1,0:T(8,128)(2,1)} %collective-permute-done.2, bf16[5,512,768]{2,1,0:T(8,128)(2,1)} %param.12, pred[]{:T(512)S(6)} %eq.23), kind=kOutput, calls=%fused_computation.35 | convolution fusion | flops 16108093440 | bytes 81264640 | tf_op jit(solution)/shard_map/pecd,efd->pecf/dot_general | solution.py:184
  1218.0 35.5 %fusion = f32[8,5,512]{2,1,0:T(8,128)S(1)} fusion(f32[5,512,8,512]{1,3,0,2:T(8,128)} %fusion.14, bf16[8,5,512,512]{3,2,1,0:T(8,128)(2,1)} %get-tuple-element.60, bf16[8,5,512,768]{3,2,1,0:T(8,128)(2,1)} %get-tuple-element.78, bf16[5,512,768]{2,1,0:T(8,128)(2,1)} %param.12, bf16[5,512,768]{2,1,0:T(8,128)(2,1)} %collective-permute-done.2, pred[]{:T(512)S(6)} %eq.23), kind=kOutput, calls=%fused_computation.3 | convolution fusion | flops 16150016000 | bytes 102318080 | tf_op jit(solution)/shard_map/pecd,efd->pecf/dot_general | solution.py:184
  1253.5 32.4 %select_reduce_fusion = f32[8,5,2048]{2,1,0:T(8,128)S(1)} fusion(f32[8,5,512]{2,1,0:T(8,128)S(1)} %fusion, s32[8,5,2048]{2,1,0:T(8,128)S(1)} %copy.94), kind=kLoop, calls=%fused_computation | loop fusion | flops 125747200 | bytes 737280 | tf_op jit(solution)/shard_map/reduce_sum | solution.py:280
  1285.9 64.8 %all_to_all.5 = f32[8,5,2048]{2,1,0:T(8,128)S(1)} all-to-all(f32[8,5,2048]{2,1,0:T(8,128)S(1)} %select_reduce_fusion), channel_id=1, replica_groups=mesh['fsdp'=2,'ep'=8] {'ep'}, dimensions={0} | all-to-all | bytes 655360 | tf_op jit(solution)/shard_map/all_to_all | solution.py:281
  1350.8 0.9 select_reduce_fusion.1
  1351.8 172.5 %collective-permute-done.5 = f32[5,768,512]{2,1,0:T(8,128)} collective-permute-done((f32[5,768,512]{2,1,0:T(8,128)}, f32[5,768,512]{2,1,0:T(8,128)}, u32[]{:S(2)}, u32[]{:S(2)}) %collective-permute-start.5) | collective-permute-done | bytes 7864352 | tf_op jit(solution)/shard_map/ppermute | solution.py:271
  1524.3 12.6 select_add_fusion
  1536.9 154.2 %collective-permute-done.3 = f32[5,768,512]{2,1,0:T(8,128)} collective-permute-done((f32[5,768,512]{2,1,0:T(8,128)}, f32[5,768,512]{2,1,0:T(8,128)}, u32[]{:S(2)}, u32[]{:S(2)}) %collective-permute-start.3) | collective-permute-done | bytes 7864352 | tf_op jit(solution)/shard_map/ppermute | solution.py:268
  1691.0 12.6 select_add_fusion.1
  1703.6 12.4 fusion.9
  1716.0 1.7 convert_bitcast_fusion.3
  1717.8 2.6 convert_bitcast_fusion.2
  1720.4 2.5 convert_bitcast_fusion.1
  1722.9 2.5 convert_bitcast_fusion
  1725.4 4.0 pad_maximum_fusion
  (51 shorter events, 3.7 us)
Async XLA Ops:
  7.2 235.9 %all-gather.6.cloned.1.call-start = ((), (), s32[]{:S(2)}) async-start(), calls=%async_computation.5 | async-start | bytes 56623104 | tf_op jit(solution)/shard_map/all_gather | solution.py:205
  7.9 438.4 %all-gather.10.cloned.1.call-start = ((), (), s32[]{:S(2)}) async-start(), calls=%async_computation.7 | async-start | bytes 28311552 | tf_op jit(solution)/shard_map/all_gather | solution.py:219
  7.9 89.4 %collective-permute-start = (bf16[5,768,512]{2,1,0:T(8,128)(2,1)}, bf16[5,768,512]{2,1,0:T(8,128)(2,1)}, u32[]{:S(2)}, u32[]{:S(2)}) collective-permute-start(bf16[5,768,512]{2,1,0:T(8,128)(2,1)} %param.11), channel_id=1, source_target_pairs={{0,8},{8,0},{1,9},{9,1},{2,10},{10,2},{3,11},{11,3},{4,12},{12,4},... | collective-permute-start | bytes 11796488 | tf_op jit(solution)/shard_map/ppermute | solution.py:206
  11.3 169.5 %collective-permute-start.1 = (bf16[5,768,512]{2,1,0:T(8,128)(2,1)}, bf16[5,768,512]{2,1,0:T(8,128)(2,1)}, u32[]{:S(2)}, u32[]{:S(2)}) collective-permute-start(bf16[5,768,512]{2,1,0:T(8,128)(2,1)} %param.13), channel_id=1, source_target_pairs={{0,8},{8,0},{1,9},{9,1},{2,10},{10,2},{3,11},{11,3},{4,12},{12,4},... | collective-permute-start | bytes 11796488 | tf_op jit(solution)/shard_map/ppermute | solution.py:207
  31.2 25.9 %copy-start.4 = (f32[2048,8]{0,1:T(8,128)S(1)}, f32[2048,8]{0,1:T(8,128)}, u32[]{:S(2)}) copy-start(f32[2048,8]{0,1:T(8,128)} %param.10) | copy-start | bytes 196612
  70.5 12.3 slice-start
  71.3 11.4 slice-start.1
  76.9 5.8 copy-start
  243.1 303.4 %all-gather.8.cloned.1.call-start = ((), (), s32[]{:S(2)}) async-start(), calls=%async_computation.6 | async-start | bytes 28311552 | tf_op jit(solution)/shard_map/all_gather | solution.py:221
  329.0 1387.1 %reduce-scatter.5.cloned.1.call-start = ((), (), s32[]{:S(2)}) async-start(), calls=%async_computation.8 | async-start | bytes 18874368 | tf_op jit(solution)/shard_map/reduce_scatter | solution.py:246
  329.5 185.0 %collective-permute-start.2 = (bf16[5,512,768]{2,1,0:T(8,128)(2,1)}, bf16[5,512,768]{2,1,0:T(8,128)(2,1)}, u32[]{:S(2)}, u32[]{:S(2)}) collective-permute-start(bf16[5,512,768]{2,1,0:T(8,128)(2,1)} %param.12), channel_id=1, source_target_pairs={{0,8},{8,0},{1,9},{9,1},{2,10},{10,2},{3,11},{11,3},{4,12},{12,4},... | collective-permute-start | bytes 11796488 | tf_op jit(solution)/shard_map/ppermute | solution.py:208
  331.2 4.1 copy-start.1
  335.3 6.2 copy-start.2
  398.0 47.7 %copy-start.5 = (s32[8,8]{1,0:T(8,128)S(1)}, s32[8,8]{1,0:T(8,128)}, u32[]{:S(2)}) copy-start(s32[8,8]{1,0:T(8,128)} %get-tuple-element.84) | copy-start | bytes 772
  781.5 936.3 %reduce-scatter.7.cloned.1.call-start = ((), (), s32[]{:S(2)}) async-start(), calls=%async_computation.9 | async-start | bytes 18874368 | tf_op jit(solution)/shard_map/reduce_scatter | solution.py:246
  907.2 813.2 %reduce-scatter.9.cloned.1.call-start = ((), (), s32[]{:S(2)}) async-start(), calls=%async_computation.10 | async-start | bytes 37748736 | tf_op jit(solution)/shard_map/reduce_scatter | solution.py:246
  982.4 740.5 %reduce-scatter.11.cloned.1.call-start = ((), (), s32[]{:S(2)}) async-start(), calls=%async_computation.11 | async-start | bytes 37748736 | tf_op jit(solution)/shard_map/reduce_scatter | solution.py:246
  1183.3 520.3 %collective-permute-start.4 = (f32[5,512,768]{2,1,0:T(8,128)}, f32[5,512,768]{2,1,0:T(8,128)}, u32[]{:S(2)}, u32[]{:S(2)}) collective-permute-start(f32[5,512,768]{2,1,0:T(8,128)} %get-tuple-element.81), channel_id=1, source_target_pairs={{0,8},{8,0},{1,9},{9,1},{2,10},{10,2},{3,11},{11,3},{4,12},{12,4},... | collective-permute-start | bytes 23592968 | tf_op jit(solution)/shard_map/ppermute | solution.py:254
  1183.3 340.9 %collective-permute-start.5 = (f32[5,768,512]{2,1,0:T(8,128)}, f32[5,768,512]{2,1,0:T(8,128)}, u32[]{:S(2)}, u32[]{:S(2)}) collective-permute-start(f32[5,768,512]{2,1,0:T(8,128)} %slice_select_fusion), channel_id=1, source_target_pairs={{0,8},{8,0},{1,9},{9,1},{2,10},{10,2},{3,11},{11,3},{4,12},{12,4},... | collective-permute-start | bytes 23592968 | tf_op jit(solution)/shard_map/ppermute | solution.py:271
  1185.4 505.7 %collective-permute-start.3 = (f32[5,768,512]{2,1,0:T(8,128)}, f32[5,768,512]{2,1,0:T(8,128)}, u32[]{:S(2)}, u32[]{:S(2)}) collective-permute-start(f32[5,768,512]{2,1,0:T(8,128)} %slice_select_fusion.1), channel_id=1, source_target_pairs={{0,8},{8,0},{1,9},{9,1},{2,10},{10,2},{3,11},{11,3},{4,12},{12,4},... | collective-permute-start | bytes 23592968 | tf_op jit(solution)/shard_map/ppermute | solution.py:268
  1218.0 132.8 %copy-start.3 = (s32[2048,8]{0,1:T(8,128)S(1)}, s32[2048,8]{0,1:T(8,128)}, u32[]{:S(2)}) copy-start(s32[2048,8]{0,1:T(8,128)} %param.9) | copy-start | bytes 196612
Sparse Core Ops, SparseCore 0:
  9.8 233.2 all-gather.5
  245.5 121.4 all-gather.9
  369.4 121.4 all-gather.7
  781.6 134.1 reduce-scatter.4
  919.1 124.2 reduce-scatter.6
  1046.9 199.8 reduce-scatter.8
  1250.3 205.4 reduce-scatter.10
